TPU v7x, 512 devices: a whole 4x8x8 slice. The times are simulated.
512 devices in a mesh: seq: 64 (over x, z, core), res: 8 (over y).
Axes of the slice: x: 4, y: 8, z: 8, core: 2. Of those that a mesh axis runs over, the one named last changes fastest.
Arguments:
- alignment_rows: bfloat16 [4096, 64, 64], P('seq', 'res'), may hold values from -6 to 6
- pair_features: bfloat16 [64, 64, 128], P('res', 'seq'), may hold values from -6 to 6
- sequence_block_count: int32 [64], P('seq'), may hold values from 16 to 64
- cluster_member_count: int32 [4096], P('seq'), may hold values from 1 to 16
- residue_present_mask: int32 [64], replicated, may hold values 0 or 1
- attention_in_weight: bfloat16 [64, 256], replicated, may hold values from -0.75 to 0.75
- attention_out_weight: bfloat16 [64, 64], replicated, may hold values from -4 to 4
- pair_bias_weight: float32 [128, 8], replicated, may hold values from -48 to 48
- outer_factor_weight: bfloat16 [64, 64], replicated, may hold values from -0.75 to 0.75
- outer_output_weight: float32 [1024, 128], replicated, may hold values from -4 to 4
- outer_product_bias: float32 [128], replicated, may hold values from -3 to 3
Outputs:
- row_attention_update: bfloat16 [4096, 64, 64], P('seq', 'res')
- pair_update: bfloat16 [64, 64, 128], P('seq', 'res')
All inputs are finite; a program needn't handle non-finite values.
Results may differ from a plain program's by a relative error of at most 0.0081.
Values may be sent and summed in bfloat16 or wider, within the bound.
A program may use at most 64 MiB of HBM per device.

v0:
```python
import math

import jax
import jax.numpy as jnp
from jax import lax
from jax.sharding import PartitionSpec as P


def from_everyone(shard, axis):
    copies = jnp.broadcast_to(shard, (lax.axis_size(axis), *shard.shape))
    return lax.all_to_all(copies, axis, split_axis=0, concat_axis=0, tiled=True)


def over_copies(shard, axis):
    everything = from_everyone(shard, axis)
    return jnp.sum(everything, axis=0)


def in_order(pieces, dim):
    pieces = jnp.moveaxis(pieces, 0, dim)
    lengths = pieces.shape
    return pieces.reshape(*lengths[:dim], lengths[dim] * lengths[dim + 1], *lengths[dim + 2 :])


def collect(shard, axis, dim):
    pieces = from_everyone(shard, axis)
    return in_order(pieces, dim)


def cut_along(shard, dim, devices):
    lengths = shard.shape
    pieces = shard.reshape(*lengths[:dim], devices, lengths[dim] // devices, *lengths[dim + 1 :])
    return jnp.moveaxis(pieces, dim, 0)


def summed_on_arrival(shard, axis, dim):
    pieces = cut_along(shard, dim, lax.axis_size(axis))
    arrived = lax.all_to_all(pieces, axis, split_axis=0, concat_axis=0, tiled=True)
    return arrived.astype(jnp.float32).sum(axis=0)


def apply_layer_norm(values):
    centre = jnp.mean(values, axis=-1, keepdims=True)
    spread = jnp.mean(jnp.square(values - centre), axis=-1, keepdims=True)
    return (values - centre) * lax.rsqrt(spread + 1e-05)


def apply_row_projection(input_rows, attention_in_weight):
    slot_count, n_res, channel_width = input_rows.shape
    normed_alignment = apply_layer_norm(input_rows.astype(jnp.float32)).astype(jnp.bfloat16)
    projected_rows = jnp.dot(
        normed_alignment.reshape(-1, channel_width),
        attention_in_weight,
        preferred_element_type=jnp.float32,
    ).reshape(slot_count, n_res, 4 * channel_width)
    return projected_rows


def split_projection_parts(projected_rows, head_count):
    channel_width = projected_rows.shape[-1] // 4
    head_dim = channel_width // head_count
    query_rows = (projected_rows[..., :channel_width] * (1.0 / math.sqrt(head_dim))).astype(
        jnp.bfloat16
    )
    key_value_pairs = projected_rows[..., channel_width : 3 * channel_width].astype(jnp.bfloat16)
    gate_activation = jax.nn.sigmoid(projected_rows[..., 3 * channel_width :])
    return (query_rows, key_value_pairs, gate_activation)


def attend(query_rows, key_value_pairs, gate_activation, full_bias, attention_out_weight):
    slot_count, n_query, channel_width = query_rows.shape
    head_count = full_bias.shape[0]
    head_dim = channel_width // head_count
    n_keys = key_value_pairs.shape[1]
    block = math.gcd(slot_count, max(1, (1 << 18) // (head_count * n_query * n_keys)))

    def one_block(pieces):
        query_blk, kv_blk = pieces
        query_heads = query_blk.reshape(block, n_query, head_count, head_dim)
        key_heads = kv_blk[..., :channel_width].reshape(block, n_keys, head_count, head_dim)
        value_heads = kv_blk[..., channel_width:].reshape(block, n_keys, head_count, head_dim)
        scores = (
            jnp.einsum(
                "bihd,bjhd->bhij", query_heads, key_heads, preferred_element_type=jnp.float32
            )
            + full_bias[None]
        )
        row_max = jnp.max(scores, axis=-1, keepdims=True)
        expo = jnp.exp(scores - row_max)
        probs = (expo / jnp.sum(expo, axis=-1, keepdims=True)).astype(jnp.bfloat16)
        context = jnp.einsum(
            "bhij,bjhd->bihd", probs, value_heads, preferred_element_type=jnp.float32
        )
        return context.reshape(block, n_query, channel_width)

    context = lax.map(
        one_block,
        (
            query_rows.reshape(-1, block, n_query, channel_width),
            key_value_pairs.reshape(-1, block, n_keys, 2 * channel_width),
        ),
    )
    context = context.reshape(slot_count, n_query, channel_width)
    gated = (gate_activation * context).astype(jnp.bfloat16)
    update = jnp.dot(
        gated.reshape(-1, channel_width), attention_out_weight, preferred_element_type=jnp.float32
    ).astype(jnp.bfloat16)
    return update.reshape(slot_count, n_query, channel_width)


def local(
    alignment_rows,
    pair_features,
    sequence_block_count,
    cluster_member_count,
    residue_present_mask,
    attention_in_weight,
    attention_out_weight,
    pair_bias_weight,
    outer_factor_weight,
    outer_output_weight,
    outer_product_bias,
):
    slot_count, local_residues, channel_width = alignment_rows.shape
    head_count = pair_bias_weight.shape[1]
    block_length = local_residues * lax.axis_size("res")
    factor_width = outer_factor_weight.shape[1] // 2
    pair_width = outer_output_weight.shape[1]
    usable = (jnp.arange(slot_count, dtype=jnp.int32) < sequence_block_count[0]).astype(jnp.float32)
    seq_weight = cluster_member_count.astype(jnp.float32) * usable
    weight_sum = over_copies(jnp.sum(seq_weight), "seq")
    key_mask = jnp.where(residue_present_mask == 1, 0.0, -1000000.0).astype(jnp.float32)
    pair_norm = apply_layer_norm(pair_features.astype(jnp.float32))
    bias_tile = jnp.einsum(
        "ijp,ph->hij", pair_norm, pair_bias_weight, precision=lax.Precision.HIGHEST
    )
    bias_local = collect(bias_tile, "seq", 2) + key_mask[None, None, :]
    flat_rows = alignment_rows.reshape(slot_count, local_residues * channel_width)
    arrived = lax.all_to_all(flat_rows, "res", split_axis=0, concat_axis=1, tiled=True).reshape(
        -1, block_length, channel_width
    )
    full_bias = collect(bias_local, "res", 1)
    query_rows, key_value_pairs, gate_activation = split_projection_parts(
        apply_row_projection(arrived, attention_in_weight), head_count
    )
    update = attend(query_rows, key_value_pairs, gate_activation, full_bias, attention_out_weight)
    returned = lax.all_to_all(
        update.reshape(-1, block_length * channel_width),
        "res",
        split_axis=1,
        concat_axis=0,
        tiled=True,
    )
    returned = returned.reshape(slot_count, local_residues, channel_width)
    row_attention_update = returned * usable.astype(jnp.bfloat16)[:, None, None]
    updated_alignment = alignment_rows.astype(jnp.float32) + row_attention_update.astype(
        jnp.float32
    )
    outer_input_norm = apply_layer_norm(updated_alignment).astype(jnp.bfloat16)
    factors = jnp.dot(
        outer_input_norm.reshape(-1, channel_width),
        outer_factor_weight,
        preferred_element_type=jnp.float32,
    ).reshape(slot_count, local_residues, 2 * factor_width)
    res_start = lax.axis_index("res") * local_residues
    res_keep = lax.dynamic_slice_in_dim(residue_present_mask, res_start, local_residues).astype(
        jnp.float32
    )[None, :, None]
    left_proj = (factors[..., :factor_width] * res_keep).astype(jnp.bfloat16)
    right_proj = (factors[..., factor_width:] * res_keep * seq_weight[:, None, None]).astype(
        jnp.bfloat16
    )
    left_all = collect(left_proj.reshape(slot_count, local_residues * factor_width), "res", 1)
    left_all = left_all.reshape(slot_count, block_length, factor_width)
    right_flat = right_proj.reshape(slot_count, local_residues * factor_width)
    weight_cube = outer_output_weight.reshape(factor_width, factor_width, pair_width)
    block = math.gcd(block_length // lax.axis_size("seq") * lax.axis_size("seq"), 16)

    def block_term(block_index):
        left_block = lax.dynamic_slice_in_dim(left_all, block_index * block, block, 1)
        outer_block = lax.dot_general(
            left_block.reshape(slot_count, block * factor_width),
            right_flat,
            (((0,), (0,)), ((), ())),
            preferred_element_type=jnp.float32,
        )
        outer_block = outer_block.reshape(block, factor_width, local_residues, factor_width)
        return jnp.einsum(
            "icjd,cdp->ijp", outer_block, weight_cube, precision=lax.Precision.HIGHEST
        )

    blocks_out = lax.map(
        block_term,
        jnp.arange(
            block_length // lax.axis_size("seq") * lax.axis_size("seq") // block, dtype=jnp.int32
        ),
    )
    summed = summed_on_arrival(
        blocks_out.reshape(
            block_length // lax.axis_size("seq") * lax.axis_size("seq"), local_residues, pair_width
        ).astype(jnp.bfloat16),
        "seq",
        0,
    )
    pair_update = (summed / weight_sum + outer_product_bias).astype(jnp.bfloat16)
    return (row_attention_update, pair_update)


def solution(mesh):
    return jax.shard_map(
        local,
        mesh=mesh,
        in_specs=(
            P("seq", "res", None),
            P("res", "seq", None),
            P("seq"),
            P("seq"),
            P(),
            P(),
            P(),
            P(),
            P(),
            P(),
            P(),
        ),
        out_specs=(P("seq", "res", None), P("seq", "res", None)),
        check_vma=False,
    )
```

profile of v0, /device:TPU:1, one launch (start us, length us, event | category | flops | bytes accessed | tf_op | source)
XLA Modules:
  0.0 144.2 jit_solution(6712411401909029182)
XLA Ops:
  0.6 0.8 convert_reduce_fusion.1
  1.5 0.9 fusion.48
  2.3 0.9 convolution_bitcast_fusion.1
  3.3 0.7 broadcast_in_dim.46
  4.0 14.8 %all-to-all-start.1 = ((f32[64,8,8,1]{2,1,3,0:T(8,128)}), f32[64,8,8,1]{2,1,3,0:T(8,128)S(1)}, u32[]{:S(2)}, u32[]{:S(2)}) async-start(f32[64,8,8,1]{2,1,3,0:T(8,128)} %broadcast_in_dim.46), calls=%async_computation.1 | async-start | bytes 524288 | tf_op jit(solution)/shard_map/all_to_all | solution.py:11
  18.9 0.7 compare_select_fusion
  20.2 1.3 fusion.55
  21.4 1.7 %all_to_all.38 = bf16[8,8,512]{2,1,0:T(8,128)(2,1)} reshape(bf16[64,8,64]{2,1,0:T(8,128)(2,1)} %param.13) | data formatting | bytes 131072 | tf_op jit(solution)/shard_map/all_to_all | solution.py:139
  23.1 7.7 %all-to-all-done.1 = f32[64,8,8,1]{2,1,3,0:T(8,128)S(1)} async-done(((f32[64,8,8,1]{2,1,3,0:T(8,128)}), f32[64,8,8,1]{2,1,3,0:T(8,128)S(1)}, u32[]{:S(2)}, u32[]{:S(2)}) %all-to-all-start.1) | async-done | bytes 16416 | tf_op jit(solution)/shard_map/all_to_all | solution.py:11
  30.8 6.8 %all-to-all-start = ((bf16[8,8,512]{2,1,0:T(8,128)(2,1)}), bf16[8,8,512]{2,1,0:T(8,128)(2,1)S(1)}, u32[]{:S(2)}, u32[]{:S(2)}) async-start(bf16[8,8,512]{2,1,0:T(8,128)(2,1)} %all_to_all.38), calls=%async_computation | async-start | bytes 131072 | tf_op jit(solution)/shard_map/all_to_all | solution.py:139
  37.6 0.1 bitcast_add_fusion
  37.8 0.1 copy.88
  37.9 0.8 reshape.231
  38.8 6.1 %all-to-all-done = bf16[8,8,512]{2,1,0:T(8,128)(2,1)S(1)} async-done(((bf16[8,8,512]{2,1,0:T(8,128)(2,1)}), bf16[8,8,512]{2,1,0:T(8,128)(2,1)S(1)}, u32[]{:S(2)}, u32[]{:S(2)}) %all-to-all-start) | async-done | bytes 65568 | tf_op jit(solution)/shard_map/all_to_all | solution.py:139
  44.9 3.4 %all-to-all-start.2 = ((f32[8,1,4096]{2,1,0:T(1,128)}), f32[8,1,4096]{2,1,0:T(1,128)S(1)}, u32[]{:S(2)}, u32[]{:S(2)}) async-start(f32[8,1,4096]{2,1,0:T(1,128)} %reshape.231), calls=%async_computation.2 | async-start | bytes 262144 | tf_op jit(solution)/shard_map/all_to_all | solution.py:11
  48.5 0.1 reduce_sum.91
  48.6 0.3 multiply_reduce_fusion.1
  48.9 0.3 fusion.57
  49.2 0.1 fusion.56
  49.3 0.1 copy.86
  49.5 0.1 copy.85
  49.7 0.1 copy.84
  49.8 6.3 %all-to-all-done.2 = f32[8,1,4096]{2,1,0:T(1,128)S(1)} async-done(((f32[8,1,4096]{2,1,0:T(1,128)}), f32[8,1,4096]{2,1,0:T(1,128)S(1)}, u32[]{:S(2)}, u32[]{:S(2)}) %all-to-all-start.2) | async-done | bytes 131104 | tf_op jit(solution)/shard_map/all_to_all | solution.py:11
  56.1 0.5 broadcast.134
  56.7 1.0 reduce.4
  57.7 0.1 copy.90
  57.9 2.3 %fusion.58 = (f32[8,8,64]{2,1,0:T(8,128)S(1)}, f32[8,8,64,64]{2,3,1,0:T(8,128)}) fusion(f32[8,64,64]{1,2,0:T(8,128)S(1)} %copy.90, bf16[8,64,64]{1,2,0:T(8,128)(2,1)S(1)} %copy.86, bf16[8,64,64]{1,2,0:T(8,128)(2,1)S(1)} %copy.85), kind=kOutput, calls=%fused_computation.81 | convolution fusion | flops 4980799 | bytes 1327104 | tf_op jit(solution)/shard_map/while/body/eval_jaxpr/sub | solution.py:89
  60.2 2.0 %convolution_bitcast_fusion = f32[8,64,64]{1,2,0:T(8,128)S(1)} fusion(f32[8,8,64,64]{2,3,1,0:T(8,128)} %get-tuple-element.79, f32[8,8,64]{2,1,0:T(8,128)S(1)} %get-tuple-element.78, bf16[8,64,64]{1,2,0:T(8,128)(2,1)S(1)} %copy.84), kind=kOutput, calls=%fused_computation.14 | convolution fusion | flops 4718592 | bytes 1261568 | tf_op jit(solution)/shard_map/while/body/eval_jaxpr/bhij,bjhd->bihd/dot_general | solution.py:91
  62.2 0.1 copy.92
  62.3 0.2 fusion.21
  62.5 0.2 convolution_convert_fusion
  62.7 0.1 copy.93
  62.8 0.1 all_to_all.42
  63.0 0.7 copy.94
  63.6 3.4 %all-to-all-start.3 = ((bf16[8,8,512]{2,0,1:T(8,128)(2,1)}), bf16[8,8,512]{2,0,1:T(8,128)(2,1)S(1)}, u32[]{:S(2)}, u32[]{:S(2)}) async-start(bf16[8,8,512]{2,0,1:T(8,128)(2,1)} %copy.94), calls=%async_computation.3 | async-start | bytes 131072 | tf_op jit(solution)/shard_map/all_to_all | solution.py:147
  67.1 7.0 %all-to-all-done.3 = bf16[8,8,512]{2,0,1:T(8,128)(2,1)S(1)} async-done(((bf16[8,8,512]{2,0,1:T(8,128)(2,1)}), bf16[8,8,512]{2,0,1:T(8,128)(2,1)S(1)}, u32[]{:S(2)}, u32[]{:S(2)}) %all-to-all-start.3) | async-done | bytes 65568 | tf_op jit(solution)/shard_map/all_to_all | solution.py:147
  74.1 0.1 reshape.220
  74.3 0.2 fusion.23
  74.5 0.2 multiply_reduce_fusion
  74.8 0.2 multiply_convert_fusion
  75.0 0.3 fusion.40
  75.5 0.7 broadcast_in_dim.51
  76.2 3.4 %all-to-all-start.4 = ((bf16[8,64,256]{2,1,0:T(8,128)(2,1)}), bf16[8,64,256]{2,1,0:T(8,128)(2,1)S(1)}, u32[]{:S(2)}, u32[]{:S(2)}) async-start(bf16[8,64,256]{2,1,0:T(8,128)(2,1)} %broadcast_in_dim.51), calls=%async_computation.4 | async-start | bytes 524288 | tf_op jit(solution)/shard_map/all_to_all | solution.py:11
  79.6 9.2 %all-to-all-done.4 = bf16[8,64,256]{2,1,0:T(8,128)(2,1)S(1)} async-done(((bf16[8,64,256]{2,1,0:T(8,128)(2,1)}), bf16[8,64,256]{2,1,0:T(8,128)(2,1)S(1)}, u32[]{:S(2)}, u32[]{:S(2)}) %all-to-all-start.4) | async-done | bytes 262176 | tf_op jit(solution)/shard_map/all_to_all | solution.py:11
  88.9 1.2 broadcast_in_dim.52
  90.1 10.9 %all-to-all-start.6 = ((f32[64,1,1]{2,1,0:T(1,128)}), f32[64,1,1]{2,1,0:T(1,128)S(1)}, u32[]{:S(2)}, u32[]{:S(2)}) async-start(f32[64,1,1]{2,1,0:T(1,128)} %broadcast_in_dim.52), calls=%async_computation.6 | async-start | bytes 65536 | tf_op jit(solution)/shard_map/all_to_all | solution.py:11
  101.0 0.3 copy.98
  101.3 20.8 %while.2 = (s32[]{:T(128)}, bf16[4,16,8,128]{3,2,1,0:T(8,128)(2,1)}, s32[4]{0:T(128)S(1)}, bf16[64,64,32]{0,2,1:T(8,128)(2,1)S(1)}, bf16[64,256]{0,1:T(8,128)(2,...) while((s32[]{:T(128)}, bf16[4,16,8,128]{3,2,1,0:T(8,128)(2,1)}, ...), condition=%wide.region_9.10_spmd, body=%wide.region_8.9_spmd.sunk | while | flops 218103808 | bytes 1835683 | solution.py:192
  101.3 0.6 dynamic_slice.25
  102.6 0.4 fusion.77
  103.0 3.5 %fusion.78 = bf16[4,16,8,128]{3,2,1,0:T(8,128)(2,1)} fusion(bf16[4,16,8,128]{3,2,1,0:T(8,128)(2,1)} %get-tuple-element.128, s32[]{:T(128)} %get-tuple-element.127, f32[16,32,8,32]{3,1,2,0:T(8,128)S(1)} %fusion.77, f32[32,32,128]{2,1,0:T(8,128)S(1)} %get-tuple-element.142), kind=kOutput, calls=%fused_computation.3.clone.1 | convolution fusion | flops 201326592 | bytes 1114624 | tf_op jit(solution)/shard_map/while/body/eval_jaxpr/icjd,cdp->ijp/dot_general | solution.py:188
  106.5 0.6 dynamic_slice.25
  107.8 0.5 fusion.77
  108.2 3.5 %fusion.78 = bf16[4,16,8,128]{3,2,1,0:T(8,128)(2,1)} fusion(bf16[4,16,8,128]{3,2,1,0:T(8,128)(2,1)} %get-tuple-element.128, s32[]{:T(128)} %get-tuple-element.127, f32[16,32,8,32]{3,1,2,0:T(8,128)S(1)} %fusion.77, f32[32,32,128]{2,1,0:T(8,128)S(1)} %get-tuple-element.142), kind=kOutput, calls=%fused_computation.3.clone.1 | convolution fusion | flops 201326592 | bytes 1114624 | tf_op jit(solution)/shard_map/while/body/eval_jaxpr/icjd,cdp->ijp/dot_general | solution.py:188
  111.7 0.6 dynamic_slice.25
  113.0 0.5 fusion.77
  113.4 3.5 %fusion.78 = bf16[4,16,8,128]{3,2,1,0:T(8,128)(2,1)} fusion(bf16[4,16,8,128]{3,2,1,0:T(8,128)(2,1)} %get-tuple-element.128, s32[]{:T(128)} %get-tuple-element.127, f32[16,32,8,32]{3,1,2,0:T(8,128)S(1)} %fusion.77, f32[32,32,128]{2,1,0:T(8,128)S(1)} %get-tuple-element.142), kind=kOutput, calls=%fused_computation.3.clone.1 | convolution fusion | flops 201326592 | bytes 1114624 | tf_op jit(solution)/shard_map/while/body/eval_jaxpr/icjd,cdp->ijp/dot_general | solution.py:188
  116.9 0.6 dynamic_slice.25
  118.2 0.5 fusion.77
  118.6 3.5 %fusion.78 = bf16[4,16,8,128]{3,2,1,0:T(8,128)(2,1)} fusion(bf16[4,16,8,128]{3,2,1,0:T(8,128)(2,1)} %get-tuple-element.128, s32[]{:T(128)} %get-tuple-element.127, f32[16,32,8,32]{3,1,2,0:T(8,128)S(1)} %fusion.77, f32[32,32,128]{2,1,0:T(8,128)S(1)} %get-tuple-element.142), kind=kOutput, calls=%fused_computation.3.clone.1 | convolution fusion | flops 201326592 | bytes 1114624 | tf_op jit(solution)/shard_map/while/body/eval_jaxpr/icjd,cdp->ijp/dot_general | solution.py:188
  122.1 10.3 %all-to-all-start.5 = ((bf16[64,1,8,128]{3,2,1,0:T(8,128)(2,1)}), bf16[64,1,8,128]{3,2,1,0:T(8,128)(2,1)S(1)}, u32[]{:S(2)}, u32[]{:S(2)}) async-start(bf16[64,1,8,128]{3,2,1,0:T(8,128)(2,1)} %bitcast.35), calls=%async_computation.5 | async-start | bytes 262144 | tf_op jit(solution)/shard_map/all_to_all | solution.py:38
  132.5 0.7 reduce_sum.100
  133.2 9.6 %all-to-all-done.5 = bf16[64,1,8,128]{3,2,1,0:T(8,128)(2,1)S(1)} async-done(((bf16[64,1,8,128]{3,2,1,0:T(8,128)(2,1)}), bf16[64,1,8,128]{3,2,1,0:T(8,128)(2,1)S(1)}, u32[]{:S(2)}, u32[]{:S(2)}) %all-to-all-start.5) | async-done | bytes 131104 | tf_op jit(solution)/shard_map/all_to_all | solution.py:38
  142.9 1.3 fusion.51
  (38 shorter events, 0.9 us)
Async XLA Ops:
  0.6 48.3 %copy-start = (bf16[64,256]{1,0:T(8,128)(2,1)S(1)}, bf16[64,256]{1,0:T(8,128)(2,1)}, u32[]{:S(2)}) copy-start(bf16[64,256]{1,0:T(8,128)(2,1)} %param.18) | copy-start | bytes 98308
  4.0 26.8 %all-to-all-start.1 = ((f32[64,8,8,1]{2,1,3,0:T(8,128)}), f32[64,8,8,1]{2,1,3,0:T(8,128)S(1)}, u32[]{:S(2)}, u32[]{:S(2)}) async-start(f32[64,8,8,1]{2,1,3,0:T(8,128)} %broadcast_in_dim.46), calls=%async_computation.1 | async-start | bytes 524288 | tf_op jit(solution)/shard_map/all_to_all | solution.py:11
  30.8 14.1 %all-to-all-start = ((bf16[8,8,512]{2,1,0:T(8,128)(2,1)}), bf16[8,8,512]{2,1,0:T(8,128)(2,1)S(1)}, u32[]{:S(2)}, u32[]{:S(2)}) async-start(bf16[8,8,512]{2,1,0:T(8,128)(2,1)} %all_to_all.38), calls=%async_computation | async-start | bytes 131072 | tf_op jit(solution)/shard_map/all_to_all | solution.py:139
  44.9 11.3 %all-to-all-start.2 = ((f32[8,1,4096]{2,1,0:T(1,128)}), f32[8,1,4096]{2,1,0:T(1,128)S(1)}, u32[]{:S(2)}, u32[]{:S(2)}) async-start(f32[8,1,4096]{2,1,0:T(1,128)} %reshape.231), calls=%async_computation.2 | async-start | bytes 262144 | tf_op jit(solution)/shard_map/all_to_all | solution.py:11
  60.1 2.3 %copy-start.5 = (bf16[64,64]{1,0:T(8,128)(2,1)S(1)}, bf16[64,64]{1,0:T(8,128)(2,1)}, u32[]{:S(2)}) copy-start(bf16[64,64]{1,0:T(8,128)(2,1)} %param.19) | copy-start | bytes 24580
  60.2 6.9 %copy-start.7 = (s32[64]{0:T(128)S(1)}, s32[64]{0:T(128)}, u32[]{:S(2)}) copy-start(s32[64]{0:T(128)} %param.17) | copy-start | bytes 772
  62.2 12.1 %copy-start.2 = (bf16[64,8,64]{2,1,0:T(8,128)(2,1)S(1)}, bf16[64,8,64]{2,1,0:T(8,128)(2,1)}, u32[]{:S(2)}) copy-start(bf16[64,8,64]{2,1,0:T(8,128)(2,1)} %param.13) | copy-start | bytes 196612
  62.2 12.8 %copy-start.4 = (bf16[64,64]{1,0:T(8,128)(2,1)S(1)}, bf16[64,64]{1,0:T(8,128)(2,1)}, u32[]{:S(2)}) copy-start(bf16[64,64]{1,0:T(8,128)(2,1)} %param.21) | copy-start | bytes 24580
  63.6 10.5 %all-to-all-start.3 = ((bf16[8,8,512]{2,0,1:T(8,128)(2,1)}), bf16[8,8,512]{2,0,1:T(8,128)(2,1)S(1)}, u32[]{:S(2)}, u32[]{:S(2)}) async-start(bf16[8,8,512]{2,0,1:T(8,128)(2,1)} %copy.94), calls=%async_computation.3 | async-start | bytes 131072 | tf_op jit(solution)/shard_map/all_to_all | solution.py:147
  67.0 34.3 %copy-start.1 = (f32[1024,128]{1,0:T(8,128)S(1)}, f32[1024,128]{1,0:T(8,128)}, u32[]{:S(2)}) copy-start(f32[1024,128]{1,0:T(8,128)} %param.22) | copy-start | bytes 1572868
  74.5 26.8 %copy-start.3 = (bf16[64,8,64]{2,1,0:T(8,128)(2,1)}, bf16[64,8,64]{2,1,0:T(8,128)(2,1)S(1)}, u32[]{:S(2)}) copy-start(bf16[64,8,64]{2,1,0:T(8,128)(2,1)S(1)} %get-tuple-element.71) | copy-start | bytes 196612
  76.2 12.7 %all-to-all-start.4 = ((bf16[8,64,256]{2,1,0:T(8,128)(2,1)}), bf16[8,64,256]{2,1,0:T(8,128)(2,1)S(1)}, u32[]{:S(2)}, u32[]{:S(2)}) async-start(bf16[8,64,256]{2,1,0:T(8,128)(2,1)} %broadcast_in_dim.51), calls=%async_computation.4 | async-start | bytes 524288 | tf_op jit(solution)/shard_map/all_to_all | solution.py:11
  90.1 32.0 %all-to-all-start.6 = ((f32[64,1,1]{2,1,0:T(1,128)}), f32[64,1,1]{2,1,0:T(1,128)S(1)}, u32[]{:S(2)}, u32[]{:S(2)}) async-start(f32[64,1,1]{2,1,0:T(1,128)} %broadcast_in_dim.52), calls=%async_computation.6 | async-start | bytes 65536 | tf_op jit(solution)/shard_map/all_to_all | solution.py:11
  101.3 41.6 %copy-start.6 = (f32[128]{0:T(128)S(1)}, f32[128]{0:T(128)}, u32[]{:S(2)}) copy-start(f32[128]{0:T(128)} %param.23) | copy-start | bytes 1540
  122.1 20.7 %all-to-all-start.5 = ((bf16[64,1,8,128]{3,2,1,0:T(8,128)(2,1)}), bf16[64,1,8,128]{3,2,1,0:T(8,128)(2,1)S(1)}, u32[]{:S(2)}, u32[]{:S(2)}) async-start(bf16[64,1,8,128]{3,2,1,0:T(8,128)(2,1)} %bitcast.35), calls=%async_computation.5 | async-start | bytes 262144 | tf_op jit(solution)/shard_map/all_to_all | solution.py:38
where the time goes:
time: 145 us; the launch traced here: 144 us
  starting transfers between devices  53 us (37%)
  waiting for transfers between devices  46 us (32%)
  matrix products  21.8 us (15%)
  local copies, waits for them, and re-layouts  10.9 us (8%)
  other arithmetic  8.25 us (6%)
  loops' own time  2.62 us (2%)
  between operations  1.66 us (1%)
    all_to_all x4, starting transfers between devices, from_everyone(): return lax.all_to_all(copies, axis, split_axis=0, concat_axis=0, tiled=True)  32.5 us
    all_to_all x4, waiting for transfers between devices, from_everyone(): return lax.all_to_all(copies, axis, split_axis=0, concat_axis=0, tiled=True)  23.3 us
    dot_general x4, matrix products, block_term(): jnp.einsum('icjd,cdp->ijp', outer_block, weight_cube, precision=lax.Preci...  14 us
    all_to_all x1, starting transfers between devices, summed_on_arrival(): lax.all_to_all(pieces, axis, split_axis=0, concat_axis=0, tiled=True)  10.3 us
    all_to_all x1, waiting for transfers between devices, summed_on_arrival(): lax.all_to_all(pieces, axis, split_axis=0, concat_axis=0, tiled=True)  9.59 us
    all_to_all x1, waiting for transfers between devices, local(): lax.all_to_all(update.reshape(-1, block_length * channel_width), 'res', s...  7.03 us
    all_to_all x1, starting transfers between devices, local(): lax.all_to_all(flat_rows, 'res', split_axis=0, concat_axis=1, tiled=True)  6.82 us
    all_to_all x1, waiting for transfers between devices, local(): lax.all_to_all(flat_rows, 'res', split_axis=0, concat_axis=1, tiled=True)  6.09 us
  transfers between devices with their start and end apart: 7, of which 6 were waited for; matrix products, arithmetic and copies ran while one was open for 17% of the time, Pallas kernels for 0%

commit v1 on v0

v1 whole, which is shorter than its diff:
```python
import functools
import math

import jax
import jax.numpy as jnp
from jax import lax
from jax.experimental import pallas as pl
from jax.experimental.pallas import tpu as pltpu
from jax.sharding import PartitionSpec as P

F32 = jnp.float32
BF16 = jnp.bfloat16
MESH = pl.DeviceIdType.MESH
HI = lax.Precision.HIGHEST
N_SEQ, N_RES = 64, 8
NX, NZ, NC = 4, 8, 2


def iota(shape, dim):
    return lax.broadcasted_iota(jnp.int32, shape, dim)


def where(cond, a, b):
    return jnp.where(cond, a, b)


def mm(a, b):
    return jnp.dot(a, b, preferred_element_type=F32)


def mm_nt(a, b, precision=None):
    dims = (((1,), (1,)), ((), ()))
    return lax.dot_general(a, b, dims, precision=precision, preferred_element_type=F32)


def mm_tn(a, b):
    return mm(a.T, b)


def norm_rows(v, axis):
    centre = jnp.mean(v, axis=axis, keepdims=True)
    spread = jnp.mean(jnp.square(v - centre), axis=axis, keepdims=True)
    return (v - centre) * lax.rsqrt(spread + 1e-05)


def wait_bytes(ref, sem):
    pltpu.make_async_copy(ref, ref, sem).wait()


def kernel(
    x_ref, pf_ref, cnt_ref, cmc_ref, mask_ref, win_ref, wout_ref, wb_ref, wf_ref, ow_ref, ob_ref,
    upd_ref, pair_ref,
    xs, xr, bs, br, b2s, b2r, ls, lr, rs, rr, us, ur, ps, pr, w1s, w1r, w2s, w2r,
    tt, w4, bias2, rows,
    x_ss, x_rs, b_ss, b_rs, b2_ss, b2_rs, l_ss, l_rs, r_ss, r_rs, u_ss, u_rs, p_ss, p_rs,
    w1_ss, w1_rs, w2_ss, w2_rs,
):
    b = lax.axis_index("seq")
    r = lax.axis_index("res")
    bx = b // (NZ * NC)
    bz = (b // NC) % NZ
    bc = b % NC

    def res_peer(k):
        return (r + k) % N_RES

    def seq_peer(k):
        kc = 1 - k % 2
        tz = (k // 2) % NZ
        tx = k // (NZ * NC)
        kz = NZ // 2 + ((tz + 1) // 2) * (1 - 2 * (tz % 2))
        kx = NX // 2 + ((tx + 1) // 2) * (1 - 2 * (tx % 2))
        return ((bx + kx) % NX) * (NZ * NC) + ((bz + kz) % NZ) * NC + (bc + kc) % NC

    barrier = pltpu.get_barrier_semaphore()

    def greet(k, carry):
        pl.semaphore_signal(barrier, inc=1, device_id=(seq_peer(k), r), device_id_type=MESH)
        return carry

    lax.fori_loop(0, N_SEQ - 1, greet, 0)
    for k in range(1, N_RES):
        pl.semaphore_signal(barrier, inc=1, device_id=(b, res_peer(k)), device_id_type=MESH)

    pn = norm_rows(pf_ref[...].astype(F32), -1)
    pn = jnp.concatenate([pn] * 16, axis=0)
    pn = where((iota((128, 128), 0) // 8) % 8 == r, pn, 0.0)
    full = mm_nt(wb_ref[...].T, pn, HI)
    low = iota((4, 128), 1) < 64
    tile = where(low, full[0:4], full[4:8])
    bs[...] = tile
    br[pl.ds(r, 1)] = tile[None]

    flat = x_ref[...].astype(F32).reshape(512, 64).astype(BF16)
    dup = where(iota((64, 128), 1) % 64 == iota((64, 128), 0), 1.0, 0.0).astype(BF16)
    wide = mm(flat, dup).reshape(32, 2, 8, 128)
    pairs = where(iota((32, 8, 128), 2) < 64, wide[:, 0], wide[:, 1])
    xs[...] = pairs.reshape(8, 4, 8, 128).astype(BF16)
    xr[pl.ds(r, 1)] = xs[pl.ds(r, 1)]

    count = cnt_ref[0]
    total = jnp.float32(0.0)
    for s in range(64):
        total = total + where(s < count, cmc_ref[s], 0).astype(F32)
    w1s[...] = jnp.full((8, 128), 1.0, F32) * total
    w1r[pl.ds(bz, 1)] = w1s[...][None]
    use = []
    weight = []
    for s in range(8):
        slot = r * 8 + s
        on = where(slot < count, 1.0, 0.0)
        use.append(on)
        weight.append(cmc_ref[slot].astype(F32) * on)

    row = jnp.broadcast_to(mask_ref[...].astype(F32), (64, 64))
    keep = jnp.sum(where(iota((64, 64), 0) == iota((64, 64), 1), row, 0.0), axis=1, keepdims=True)
    key_mask = where(keep == 1.0, 0.0, -1000000.0)

    lane_u = iota((64, 128), 1) // 32
    parts = []
    for sp in range(2):
        part = jnp.zeros((64, 128), F32)
        for u in range(4):
            part = where(lane_u == u, weight[2 * u + sp], part)
        parts.append(part * keep)
    scale_r = jnp.concatenate(parts, axis=0)

    winT = win_ref[...].astype(F32).T.astype(BF16)
    woutT = wout_ref[...].astype(F32).T.astype(BF16)
    wout2 = mm(wout_ref[...], dup).astype(BF16)
    e_left = where(iota((64, 256), 0) == iota((64, 256), 1) // 8, 1.0, 0.0).astype(BF16)
    e_right = where(iota((64, 128), 0) == 32 + iota((64, 128), 1) % 32, 1.0, 0.0).astype(BF16)
    wl = mm(wf_ref[...], e_left).astype(BF16)
    wr = mm(wf_ref[...], e_right).astype(BF16)
    for c in range(32):
        block = ow_ref[pl.ds(c * 32, 32), :].astype(BF16)
        for q in range(4):
            w4[c // 2, pl.ds(q * 32, 32), pl.ds((c % 2) * 128, 128)] = block

    pl.semaphore_wait(barrier, N_SEQ - 1 + N_RES - 1)

    def send(src, dst, ss, rsem, dev):
        pltpu.make_async_remote_copy(
            src_ref=src, dst_ref=dst, send_sem=ss, recv_sem=rsem, device_id=dev, device_id_type=MESH
        ).start()

    far_first = (4, 3, 5, 2, 6, 1, 7)
    for k in far_first:
        send(bs, br.at[r], b_ss, b_rs, (b, res_peer(k)))
    for k in far_first:
        p = res_peer(k)
        send(xs.at[p], xr.at[r], x_ss, x_rs, (b, p))
    for k in far_first:
        peer = bx * (NZ * NC) + ((bz + k) % NZ) * NC + bc
        send(w1s, w1r.at[bz], w1_ss, w1_rs, (peer, r))

    wait_bytes(br.at[pl.ds(0, 7)], b_rs)
    tile2 = jnp.sum(br[...], axis=0)
    b2s[...] = tile2
    b2r[pl.ds(b, 1)] = tile2[None]

    def spread(k, carry):
        send(b2s, b2r.at[b], b2_ss, b2_rs, (seq_peer(k), r))
        return carry

    lax.fori_loop(0, N_SEQ - 1, spread, 0)

    wait_bytes(xr.at[pl.ds(0, 7)], x_rs)
    eye2 = where(iota((64, 128), 1) % 64 == iota((64, 128), 0), 1.0, 0.0).astype(BF16)
    half = iota((64, 128), 1) < 64
    xT = []
    for u in range(4):
        rows_u = xr[:, u].astype(F32).reshape(64, 128)
        both = jnp.concatenate([where(half, rows_u, 0.0), where(half, 0.0, rows_u)], axis=0)
        xT.append(mm_nt(eye2, both.astype(BF16)))
    xT = jnp.concatenate(xT, axis=1)
    nT = norm_rows(xT, 0).astype(BF16)
    proj = mm(winT, nT)
    qT = (proj[0:64] * (1.0 / math.sqrt(8))).astype(BF16).astype(F32)
    kT = proj[64:128].astype(BF16)
    vT = proj[128:192].astype(BF16)
    gate = jax.nn.sigmoid(proj[192:256])

    wait_bytes(w1r.at[pl.ds(0, 7)], w1_rs)
    w2 = jnp.sum(w1r[...], axis=0)
    w2s[...] = w2
    mine2 = bx * NC + bc
    w2r[pl.ds(mine2, 1)] = w2[None]
    for k in range(1, NX * NC):
        px = (bx + k // NC) % NX
        pc = (bc + k % NC) % NC
        send(w2s, w2r.at[mine2], w2_ss, w2_rs, (px * (NZ * NC) + bz * NC + pc, r))

    wait_bytes(b2r.at[pl.ds(0, N_SEQ - 1)], b2_rs)
    for hp in range(4):
        v = b2r[:, hp, :] + key_mask
        v2 = pltpu.roll(v, 64, 1)
        bias2[:, pl.ds(hp * 128, 128)] = where(half, v, v2)
        bias2[:, pl.ds((hp + 4) * 128, 128)] = where(half, v2, v)

    half2 = iota((64, 256), 1) % 128 < 64
    rowblk = iota((64, 128), 0) // 8
    gated = []
    for u in range(4):
        lanes = slice(u * 128, (u + 1) * 128)
        k_rows = kT[:, lanes].T
        q_u = qT[:, lanes]
        ctx = []
        for h in range(0, 8, 2):
            q2 = jnp.concatenate(
                [where(rowblk == h, q_u, 0.0), where(rowblk == h + 1, q_u, 0.0)], axis=1
            ).astype(BF16)
            sc = mm(k_rows, q2)
            sc = where(half2, sc[0:64], sc[64:128]) + bias2[:, pl.ds(h * 128, 256)]
            ex = jnp.exp(sc - jnp.max(sc, axis=0, keepdims=True))
            pb = ex * (1.0 / jnp.sum(ex, axis=0, keepdims=True))
            p2 = jnp.concatenate([where(half2, pb, 0.0), where(half2, 0.0, pb)], axis=0)
            cx = mm(vT[h * 8 : h * 8 + 16, lanes], p2.astype(BF16))
            ctx.append(cx[0:8, 0:128])
            ctx.append(cx[8:16, 128:256])
        gated.append((gate[:, lanes] * jnp.concatenate(ctx, axis=0)).astype(BF16))
    gT = jnp.concatenate(gated, axis=1)
    uT = mm(woutT, gT).astype(BF16).astype(F32)
    slot_lane = iota((1, 512), 1) // 64
    use_lane = jnp.zeros((1, 512), F32)
    for s in range(8):
        use_lane = where(slot_lane == s, use[s], use_lane)
    oT = norm_rows(xT + uT * use_lane, 0).astype(BF16)

    lane_s = iota((64, 256), 1) % 8
    left = jnp.zeros((64, 256), F32)
    right = jnp.zeros((128, 128), F32)
    lane_u2 = iota((128, 128), 1) // 32
    for u in range(4):
        o_rows = oT[:, u * 128 : (u + 1) * 128].T
        zl = mm(o_rows, wl)
        left = where(lane_s == 2 * u, zl[0:64], where(lane_s == 2 * u + 1, zl[64:128], left))
        right = where(lane_u2 == u, mm(o_rows, wr), right)
    right = right * scale_r
    for p in range(8):
        for sp in range(2):
            rs[p, sp] = right[sp * 64 + p * 8 : sp * 64 + p * 8 + 8].astype(BF16)
    rr[pl.ds(r, 1)] = rs[pl.ds(r, 1)]
    for k in far_first:
        p = res_peer(k)
        send(rs.at[p], rr.at[r], r_ss, r_rs, (b, p))
    left = (left * keep).astype(BF16)
    ls[...] = left
    lr[pl.ds(r, 1)] = left[None]
    for k in far_first:
        send(ls, lr.at[r], l_ss, l_rs, (b, res_peer(k)))

    for u in range(4):
        g_rows = gT[:, u * 128 : (u + 1) * 128].T
        z = mm(g_rows, wout2)
        on = where(half, use[2 * u], use[2 * u + 1])
        rows_u = where(half, z[0:64], z[64:128]).astype(BF16).astype(F32) * on
        us[:, u] = rows_u.reshape(8, 8, 128).astype(BF16)
    ur[pl.ds(r, 1)] = us[pl.ds(r, 1)]
    for k in far_first:
        p = res_peer(k)
        send(us.at[p], ur.at[r], u_ss, u_rs, (b, p))

    wait_bytes(rr.at[pl.ds(0, 7)], r_rs)
    packed = rr[...].astype(F32).reshape(128, 128).astype(BF16)
    ro = iota((512, 128), 0)
    co = iota((512, 128), 1)
    same = (ro // 64 == co // 16) & (ro % 2 == (co // 8) % 2) & ((ro // 8) % 8 == co % 8)
    spread_rows = mm(where(same, 1.0, 0.0).astype(BF16), packed)
    right_all = where((ro // 2) % 4 == co // 32, spread_rows, 0.0).astype(BF16)

    def times_weight(g, carry):
        t = mm(right_all, w4[g])
        for src in range(8):
            for j in range(8):
                a = src * 64 + j * 8
                v = jnp.concatenate([t[a : a + 8, 0:128], t[a : a + 8, 128:256]], axis=0)
                tt[j // 2, src, g, :, pl.ds((j % 2) * 128, 128)] = v.astype(BF16)
        return carry

    lax.fori_loop(0, 16, times_weight, 0)

    wait_bytes(lr.at[pl.ds(0, 7)], l_rs)
    for jp in range(4):
        acc = jnp.zeros((64, 256), F32)
        for src in range(8):
            acc = acc + mm(lr[src], tt[jp, src].reshape(256, 256))
        rows[pl.ds(2 * jp, 64, stride=8), :] = acc[:, 0:128]
        rows[pl.ds(2 * jp + 1, 64, stride=8), :] = acc[:, 128:256]
    ps[...] = rows[...].reshape(64, 8, 128).astype(BF16)
    pr[pl.ds(b, 1)] = ps[pl.ds(b, 1)]

    def scatter(k, carry):
        p = seq_peer(k)
        send(ps.at[p], pr.at[b], p_ss, p_rs, (p, r))
        return carry

    lax.fori_loop(0, N_SEQ - 1, scatter, 0)

    wait_bytes(ur.at[pl.ds(0, 7)], u_rs)
    back = ur[...].astype(F32).reshape(256, 128).astype(BF16)
    for sp in range(2):
        pick = where(iota((128, 64), 0) == iota((128, 64), 1) + 64 * sp, 1.0, 0.0).astype(BF16)
        upd_ref[:, sp] = mm(back, pick).reshape(32, 8, 64).astype(BF16)
    wait_bytes(w2r.at[pl.ds(0, 7)], w2_rs)
    weight_sum = jnp.sum(w2r[...], axis=0)

    wait_bytes(pr.at[pl.ds(0, N_SEQ - 1)], p_rs)
    summed = jnp.sum(pr[...].astype(F32), axis=0)
    pair_ref[...] = (summed / weight_sum + ob_ref[...]).astype(BF16)

    wait_bytes(xr.at[pl.ds(0, 7)], x_ss)
    wait_bytes(br.at[pl.ds(0, 7)], b_ss)
    wait_bytes(b2r.at[pl.ds(0, N_SEQ - 1)], b2_ss)
    wait_bytes(lr.at[pl.ds(0, 7)], l_ss)
    wait_bytes(rr.at[pl.ds(0, 7)], r_ss)
    wait_bytes(ur.at[pl.ds(0, 7)], u_ss)
    wait_bytes(pr.at[pl.ds(0, N_SEQ - 1)], p_ss)
    wait_bytes(w1r.at[pl.ds(0, 7)], w1_ss)
    wait_bytes(w2r.at[pl.ds(0, 7)], w2_ss)


def local(
    alignment_rows, pair_features, sequence_block_count, cluster_member_count,
    residue_present_mask, attention_in_weight, attention_out_weight, pair_bias_weight,
    outer_factor_weight, outer_output_weight, outer_product_bias,
):
    vm = pl.BlockSpec(memory_space=pltpu.VMEM)
    sm = pl.BlockSpec(memory_space=pltpu.SMEM)
    V = pltpu.VMEM
    update, pair = pl.pallas_call(
        kernel,
        out_shape=(
            jax.ShapeDtypeStruct((32, 2, 8, 64), BF16),
            jax.ShapeDtypeStruct((8, 128), BF16),
        ),
        in_specs=[vm, vm, sm, sm, vm, vm, vm, vm, vm, vm, vm],
        out_specs=(vm, vm),
        scratch_shapes=[
            V((8, 4, 8, 128), BF16), V((8, 4, 8, 128), BF16),
            V((4, 128), F32), V((8, 4, 128), F32),
            V((4, 128), F32), V((64, 4, 128), F32),
            V((64, 256), BF16), V((8, 64, 256), BF16),
            V((8, 2, 8, 128), BF16), V((8, 2, 8, 128), BF16),
            V((8, 4, 8, 128), BF16), V((8, 4, 8, 128), BF16),
            V((64, 8, 128), BF16), V((64, 8, 128), BF16),
            V((8, 128), F32), V((8, 8, 128), F32),
            V((8, 128), F32), V((8, 8, 128), F32),
            V((4, 8, 16, 16, 256), BF16), V((16, 128, 256), BF16),
            V((64, 1024), F32), V((512, 128), F32),
        ]
        + [pltpu.SemaphoreType.DMA] * 18,
        compiler_params=pltpu.CompilerParams(collective_id=0, has_side_effects=True),
    )(
        alignment_rows,
        pair_features.reshape(8, 128),
        sequence_block_count,
        cluster_member_count,
        residue_present_mask.reshape(1, 64),
        attention_in_weight,
        attention_out_weight,
        pair_bias_weight,
        outer_factor_weight,
        outer_output_weight,
        outer_product_bias.reshape(1, 128),
    )
    return update.reshape(64, 8, 64), pair.reshape(1, 8, 128)


def solution(mesh):
    return jax.shard_map(
        local,
        mesh=mesh,
        in_specs=(
            P("seq", "res", None), P("res", "seq", None), P("seq"), P("seq"),
            P(), P(), P(), P(), P(), P(), P(),
        ),
        out_specs=(P("seq", "res", None), P("seq", "res", None)),
        check_vma=False,
    )
```

time: 145 us -> 56.1 us (0.39)
  starting transfers between devices: 53 us -> 0 us
  Pallas kernels: 0 us -> 51.7 us
  waiting for transfers between devices: 46 us -> 0 us
  matrix products: 21.8 us -> 0 us
  other arithmetic: 8.25 us -> 0 us
  local copies, waits for them, and re-layouts: 10.9 us -> 2.9 us
  loops' own time: 2.62 us -> 0 us
    all_to_all x7 -> x0, starting transfers between devices: 53 us -> none  [the longest x4 32.5 us: from_everyone(): return lax.all_to_all(copies, axis, split_axis=0, concat_axis=0, tiled=True)]
    pallas_call x0 -> x1, Pallas kernels: none -> 51.7 us  [local(): pl.pallas_call(kernel, out_shape=(jax.ShapeDtypeStruct((32, 2, 8, 64), BF...]
    all_to_all x7 -> x0, waiting for transfers between devices: 46 us -> none  [the longest x4 23.3 us: from_everyone(): return lax.all_to_all(copies, axis, split_axis=0, concat_axis=0, tiled=True)]
    dot_general x13 -> x0, matrix products: 19.5 us -> none  [the longest x4 14 us: block_term(): jnp.einsum('icjd,cdp->ijp', outer_block, weight_cube, precision=lax.Preci...]
    reduce_sum x9 -> x0, other arithmetic: 4.61 us -> none  [the longest x3 1.35 us: apply_layer_norm(): spread = jnp.mean(jnp.square(values - centre), axis=-1, keepdims=True)]
    all_to_all x6 -> x0, local copies, waits for them, and re-layouts: 3.29 us -> none  [the longest x1 1.67 us: local(): lax.all_to_all(flat_rows, 'res', split_axis=0, concat_axis=1, tiled=True)]
    broadcast_in_dim x4 -> x0, local copies, waits for them, and re-layouts: 2.7 us -> none  [from_everyone(): copies = jnp.broadcast_to(shard, (lax.axis_size(axis), *shard.shape))]
    another operation x1 -> x0, loops' own time: 2.62 us -> none  [local(): lax.map(block_term, jnp.arange(block_length // lax.axis_size('seq') * lax...]
  transfers between devices with their start and end apart: 7 -> 0, of which waited for: 6 -> 0; matrix products, arithmetic and copies ran while one was open for 17% -> 0% of each run, Pallas kernels for 0% -> 0%
where the time goes in v1:
time: 56.1 us; the launch traced here: 55.9 us
  Pallas kernels  51.7 us (92%)
  local copies, waits for them, and re-layouts  2.9 us (5%)
  between operations  1.31 us (2%)
    pallas_call x1, Pallas kernels, local(): pl.pallas_call(kernel, out_shape=(jax.ShapeDtypeStruct((32, 2, 8, 64), BF...  51.7 us
    unnamed x7, local copies, waits for them, and re-layouts  2.9 us

profile of v1, /device:TPU:1, one launch (start us, length us, event | category | flops | bytes accessed | tf_op | source)
XLA Modules:
  0.0 55.9 jit_solution(2784394618526871861)
XLA Ops:
  0.6 0.0 copy-start
  1.3 0.0 copy-done
  1.3 0.7 %copy.13.wb_ref = f32[128,8]{1,0:T(8,128)} copy(f32[128,8]{0,1:T(8,128)S(1)} %copy-done) | data formatting | bytes 8192 | tf_op args[7]
  2.0 51.7 %shard_map.122 = (bf16[32,2,8,64]{3,2,1,0:T(8,128)(2,1)}, bf16[8,128]{1,0:T(8,128)(2,1)}) custom-call(bf16[64,8,64]{2,1,0:T(8,128)(2,1)} %x_ref.1, bf16[8,128]{1,0:T(8,128)(2,1)} %bitcast.6, s32[1]{0:T(128)S(6)} %copy.16.cnt_ref, s32[64]{0:T(128)} %cmc_ref.1, s32[1,64]{1,0:T(1,128)} %bitcast.8, bf16[64,256]{1,0:T(8,128)(2,1)} %win_ref.1, ...), custom_call_target="tpu_custom_call" | custom-call | tf_op jit(solution)/shard_map/pallas_call | solution.py:331
  53.7 0.0 copy-start.1
  53.7 1.6 %copy.17 = bf16[64,8,64]{2,1,0:T(8,128)(2,1)} copy(bf16[64,8,64]{2,1,0:T(8,128)(2,1)} %bitcast.5) | data formatting | bytes 131072
  55.3 0.0 copy-done.1
  55.3 0.6 %copy.18 = bf16[1,8,128]{2,1,0:T(8,128)(2,1)} copy(bf16[1,8,128]{2,1,0:T(8,128)(2,1)S(1)} %bitcast.7) | data formatting | bytes 4096
Async XLA Ops:
  0.6 0.7 %copy-start = (f32[128,8]{0,1:T(8,128)S(1)}, f32[128,8]{0,1:T(8,128)}, u32[]{:S(2)}) copy-start(f32[128,8]{0,1:T(8,128)} %param.18) | copy-start | bytes 12292
  53.7 1.6 %copy-start.1 = (bf16[8,128]{1,0:T(8,128)(2,1)S(1)}, bf16[8,128]{1,0:T(8,128)(2,1)}, u32[]{:S(2)}) copy-start(bf16[8,128]{1,0:T(8,128)(2,1)} %get-tuple-element.5) | copy-start | bytes 6148

commit v2 on v1

--- a/solution.py
+++ b/solution.py
@@ -48,12 +48,14 @@
 
 
 def kernel(
-    x_ref, pf_ref, cnt_ref, cmc_ref, mask_ref, win_ref, wout_ref, wb_ref, wf_ref, ow_ref, ob_ref,
+    x_hbm, pf_hbm, cnt_ref, cmc_hbm, mask_hbm, win_hbm, wout_hbm, wb_hbm, wf_hbm, ow_hbm, ob_hbm,
     upd_ref, pair_ref,
+    x_ref, pf_ref, cmc_ref, mask_ref, win_ref, wout_ref, wb_ref, wf_ref, ow_ref, ob_ref,
     xs, xr, bs, br, b2s, b2r, ls, lr, rs, rr, us, ur, ps, pr, w1s, w1r, w2s, w2r,
-    tt, w4, bias2, rows,
+    tt, w4, bias2, rows, score, sums,
+    in_sems,
     x_ss, x_rs, b_ss, b_rs, b2_ss, b2_rs, l_ss, l_rs, r_ss, r_rs, u_ss, u_rs, p_ss, p_rs,
-    w1_ss, w1_rs, w2_ss, w2_rs,
+    w1_ss, w1_rs, w2_ss, w2_rs, ready,
 ):
     b = lax.axis_index("seq")
     r = lax.axis_index("res")
@@ -61,36 +63,68 @@
     bz = (b // NC) % NZ
     bc = b % NC
 
-    def res_peer(k):
-        return (r + k) % N_RES
-
-    def seq_peer(k):
-        kc = 1 - k % 2
-        tz = (k // 2) % NZ
-        tx = k // (NZ * NC)
-        kz = NZ // 2 + ((tz + 1) // 2) * (1 - 2 * (tz % 2))
-        kx = NX // 2 + ((tx + 1) // 2) * (1 - 2 * (tx % 2))
-        return ((bx + kx) % NX) * (NZ * NC) + ((bz + kz) % NZ) * NC + (bc + kc) % NC
+    px = [((bx + k) % NX) * (NZ * NC) for k in range(NX)]
+    pz = [((bz + k) % NZ) * NC for k in range(NZ)]
+    pc = [(bc + k) % NC for k in range(NC)]
+    seq_peers = [
+        px[kx] + pz[kz] + pc[kc]
+        for kx in (2, 1, 3, 0)
+        for kz in (4, 3, 5, 2, 6, 1, 7, 0)
+        for kc in (1, 0)
+        if kx + kz + kc > 0
+    ]
+    far_first = (4, 3, 5, 2, 6, 1, 7)
+    res_peers = [(r + k) % N_RES for k in far_first]
 
     barrier = pltpu.get_barrier_semaphore()
 
-    def greet(k, carry):
-        pl.semaphore_signal(barrier, inc=1, device_id=(seq_peer(k), r), device_id_type=MESH)
-        return carry
-
-    lax.fori_loop(0, N_SEQ - 1, greet, 0)
-    for k in range(1, N_RES):
-        pl.semaphore_signal(barrier, inc=1, device_id=(b, res_peer(k)), device_id_type=MESH)
+    pairs_in = (
+        (pf_hbm, pf_ref), (wb_hbm, wb_ref), (x_hbm, x_ref), (cmc_hbm, cmc_ref),
+        (mask_hbm, mask_ref), (win_hbm, win_ref), (wout_hbm, wout_ref), (wf_hbm, wf_ref),
+        (ow_hbm, ow_ref), (ob_hbm, ob_ref),
+    )
+    copies = [pltpu.make_async_copy(h, v, in_sems.at[n]) for n, (h, v) in enumerate(pairs_in)]
+
+    def signal(sem, dev):
+        pl.semaphore_signal(sem, inc=1, device_id=dev, device_id_type=MESH)
+
+    z_peers = [px[0] + pz[k] + pc[0] for k in far_first]
+    xc_peers = [px[k // NC] + pz[0] + pc[k % NC] for k in (4, 5, 2, 3, 6, 7, 1)]
+    copies[0].start()
+    copies[1].start()
+    for p in z_peers:
+        signal(barrier, (p, r))
+    for p in res_peers:
+        signal(barrier, (b, p))
+    for p in xc_peers:
+        signal(barrier, (p, r))
+    for c in copies[2:]:
+        c.start()
+    copies[0].wait()
+    copies[1].wait()
 
     pn = norm_rows(pf_ref[...].astype(F32), -1)
     pn = jnp.concatenate([pn] * 16, axis=0)
     pn = where((iota((128, 128), 0) // 8) % 8 == r, pn, 0.0)
-    full = mm_nt(wb_ref[...].T, pn, HI)
+    full = mm_nt(wb_ref[...], pn, HI)
     low = iota((4, 128), 1) < 64
     tile = where(low, full[0:4], full[4:8])
     bs[...] = tile
     br[pl.ds(r, 1)] = tile[None]
 
+    pl.semaphore_wait(barrier, 21)
+    for p in z_peers:
+        signal(ready, (p, r))
+
+    def send(src, dst, ss, rsem, dev):
+        pltpu.make_async_remote_copy(
+            src_ref=src, dst_ref=dst, send_sem=ss, recv_sem=rsem, device_id=dev, device_id_type=MESH
+        ).start()
+
+    for p in res_peers:
+        send(bs, br.at[r], b_ss, b_rs, (b, p))
+
+    copies[2].wait()
     flat = x_ref[...].astype(F32).reshape(512, 64).astype(BF16)
     dup = where(iota((64, 128), 1) % 64 == iota((64, 128), 0), 1.0, 0.0).astype(BF16)
     wide = mm(flat, dup).reshape(32, 2, 8, 128)
@@ -98,6 +132,11 @@
     xs[...] = pairs.reshape(8, 4, 8, 128).astype(BF16)
     xr[pl.ds(r, 1)] = xs[pl.ds(r, 1)]
 
+    for p in res_peers:
+        send(xs.at[p], xr.at[r], x_ss, x_rs, (b, p))
+
+    for c in copies[3:]:
+        c.wait()
     count = cnt_ref[0]
     total = jnp.float32(0.0)
     for s in range(64):
@@ -125,6 +164,18 @@
         parts.append(part * keep)
     scale_r = jnp.concatenate(parts, axis=0)
 
+    for p in z_peers:
+        send(w1s, w1r.at[bz], w1_ss, w1_rs, (p, r))
+
+    wait_bytes(br.at[pl.ds(0, 7)], b_rs)
+    tile2 = jnp.sum(br[...], axis=0)
+    b2s[...] = tile2
+    b2r[pl.ds(b, 1)] = tile2[None]
+
+    pl.semaphore_wait(ready, 7)
+    for p in seq_peers:
+        send(b2s, b2r.at[b], b2_ss, b2_rs, (p, r))
+
     winT = win_ref[...].astype(F32).T.astype(BF16)
     woutT = wout_ref[...].astype(F32).T.astype(BF16)
     wout2 = mm(wout_ref[...], dup).astype(BF16)
@@ -136,34 +187,6 @@
         block = ow_ref[pl.ds(c * 32, 32), :].astype(BF16)
         for q in range(4):
             w4[c // 2, pl.ds(q * 32, 32), pl.ds((c % 2) * 128, 128)] = block
-
-    pl.semaphore_wait(barrier, N_SEQ - 1 + N_RES - 1)
-
-    def send(src, dst, ss, rsem, dev):
-        pltpu.make_async_remote_copy(
-            src_ref=src, dst_ref=dst, send_sem=ss, recv_sem=rsem, device_id=dev, device_id_type=MESH
-        ).start()
-
-    far_first = (4, 3, 5, 2, 6, 1, 7)
-    for k in far_first:
-        send(bs, br.at[r], b_ss, b_rs, (b, res_peer(k)))
-    for k in far_first:
-        p = res_peer(k)
-        send(xs.at[p], xr.at[r], x_ss, x_rs, (b, p))
-    for k in far_first:
-        peer = bx * (NZ * NC) + ((bz + k) % NZ) * NC + bc
-        send(w1s, w1r.at[bz], w1_ss, w1_rs, (peer, r))
-
-    wait_bytes(br.at[pl.ds(0, 7)], b_rs)
-    tile2 = jnp.sum(br[...], axis=0)
-    b2s[...] = tile2
-    b2r[pl.ds(b, 1)] = tile2[None]
-
-    def spread(k, carry):
-        send(b2s, b2r.at[b], b2_ss, b2_rs, (seq_peer(k), r))
-        return carry
-
-    lax.fori_loop(0, N_SEQ - 1, spread, 0)
 
     wait_bytes(xr.at[pl.ds(0, 7)], x_rs)
     eye2 = where(iota((64, 128), 1) % 64 == iota((64, 128), 0), 1.0, 0.0).astype(BF16)
@@ -181,15 +204,26 @@
     vT = proj[128:192].astype(BF16)
     gate = jax.nn.sigmoid(proj[192:256])
 
+    half2 = iota((64, 256), 1) % 128 < 64
+    rowblk = iota((64, 128), 0) // 8
+    for u in range(4):
+        lanes = slice(u * 128, (u + 1) * 128)
+        k_rows = kT[:, lanes].T
+        q_u = qT[:, lanes]
+        for h in range(0, 8, 2):
+            q2 = jnp.concatenate(
+                [where(rowblk == h, q_u, 0.0), where(rowblk == h + 1, q_u, 0.0)], axis=1
+            ).astype(BF16)
+            sc = mm(k_rows, q2)
+            score[u, :, pl.ds(h * 128, 256)] = where(half2, sc[0:64], sc[64:128])
+
     wait_bytes(w1r.at[pl.ds(0, 7)], w1_rs)
     w2 = jnp.sum(w1r[...], axis=0)
     w2s[...] = w2
     mine2 = bx * NC + bc
     w2r[pl.ds(mine2, 1)] = w2[None]
-    for k in range(1, NX * NC):
-        px = (bx + k // NC) % NX
-        pc = (bc + k % NC) % NC
-        send(w2s, w2r.at[mine2], w2_ss, w2_rs, (px * (NZ * NC) + bz * NC + pc, r))
+    for p in xc_peers:
+        send(w2s, w2r.at[mine2], w2_ss, w2_rs, (p, r))
 
     wait_bytes(b2r.at[pl.ds(0, N_SEQ - 1)], b2_rs)
     for hp in range(4):
@@ -198,20 +232,12 @@
         bias2[:, pl.ds(hp * 128, 128)] = where(half, v, v2)
         bias2[:, pl.ds((hp + 4) * 128, 128)] = where(half, v2, v)
 
-    half2 = iota((64, 256), 1) % 128 < 64
-    rowblk = iota((64, 128), 0) // 8
     gated = []
     for u in range(4):
         lanes = slice(u * 128, (u + 1) * 128)
-        k_rows = kT[:, lanes].T
-        q_u = qT[:, lanes]
         ctx = []
         for h in range(0, 8, 2):
-            q2 = jnp.concatenate(
-                [where(rowblk == h, q_u, 0.0), where(rowblk == h + 1, q_u, 0.0)], axis=1
-            ).astype(BF16)
-            sc = mm(k_rows, q2)
-            sc = where(half2, sc[0:64], sc[64:128]) + bias2[:, pl.ds(h * 128, 256)]
+            sc = score[u, :, pl.ds(h * 128, 256)] + bias2[:, pl.ds(h * 128, 256)]
             ex = jnp.exp(sc - jnp.max(sc, axis=0, keepdims=True))
             pb = ex * (1.0 / jnp.sum(ex, axis=0, keepdims=True))
             p2 = jnp.concatenate([where(half2, pb, 0.0), where(half2, 0.0, pb)], axis=0)
@@ -241,14 +267,14 @@
         for sp in range(2):
             rs[p, sp] = right[sp * 64 + p * 8 : sp * 64 + p * 8 + 8].astype(BF16)
     rr[pl.ds(r, 1)] = rs[pl.ds(r, 1)]
-    for k in far_first:
-        p = res_peer(k)
+    for p in res_peers:
         send(rs.at[p], rr.at[r], r_ss, r_rs, (b, p))
     left = (left * keep).astype(BF16)
     ls[...] = left
     lr[pl.ds(r, 1)] = left[None]
-    for k in far_first:
-        send(ls, lr.at[r], l_ss, l_rs, (b, res_peer(k)))
+    near = (3, 5, 2, 6, 1, 7)
+    for n, k in enumerate(near):
+        send(ls, lr.at[r], l_ss, l_rs.at[n], (b, (r + k) % N_RES))
 
     for u in range(4):
         g_rows = gT[:, u * 128 : (u + 1) * 128].T
@@ -257,10 +283,6 @@
         rows_u = where(half, z[0:64], z[64:128]).astype(BF16).astype(F32) * on
         us[:, u] = rows_u.reshape(8, 8, 128).astype(BF16)
     ur[pl.ds(r, 1)] = us[pl.ds(r, 1)]
-    for k in far_first:
-        p = res_peer(k)
-        send(us.at[p], ur.at[r], u_ss, u_rs, (b, p))
-
     wait_bytes(rr.at[pl.ds(0, 7)], r_rs)
     packed = rr[...].astype(F32).reshape(128, 128).astype(BF16)
     ro = iota((512, 128), 0)
@@ -278,24 +300,40 @@
                 tt[j // 2, src, g, :, pl.ds((j % 2) * 128, 128)] = v.astype(BF16)
         return carry
 
-    lax.fori_loop(0, 16, times_weight, 0)
-
-    wait_bytes(lr.at[pl.ds(0, 7)], l_rs)
+    lax.fori_loop(0, 8, times_weight, 0, unroll=4)
+
+    before = (r + 5) % N_RES
+    after = (r + 3) % N_RES
+    wait_bytes(lr.at[0], l_rs.at[0])
+    part = lr.at[before, pl.ds(0, 32)]
+    send(part, part, l_ss, l_rs.at[6], (b, (r + 1) % N_RES))
+    wait_bytes(lr.at[0], l_rs.at[1])
+    part = lr.at[after, pl.ds(32, 32)]
+    send(part, part, l_ss, l_rs.at[7], (b, (r + 7) % N_RES))
+    for p in res_peers:
+        send(us.at[p], ur.at[r], u_ss, u_rs, (b, p))
+    lax.fori_loop(8, 16, times_weight, 0, unroll=4)
+
+    for n in range(2, 6):
+        wait_bytes(lr.at[0], l_rs.at[n])
     for jp in range(4):
         acc = jnp.zeros((64, 256), F32)
-        for src in range(8):
+        for k in (0, 1, 7, 2, 6, 3, 5):
+            src = (r + k) % N_RES
             acc = acc + mm(lr[src], tt[jp, src].reshape(256, 256))
+        sums[jp] = acc
+    wait_bytes(lr.at[0, pl.ds(0, 32)], l_rs.at[6])
+    wait_bytes(lr.at[0, pl.ds(0, 32)], l_rs.at[7])
+    last = (r + 4) % N_RES
+    for jp in range(4):
+        acc = sums[jp] + mm(lr[last], tt[jp, last].reshape(256, 256))
         rows[pl.ds(2 * jp, 64, stride=8), :] = acc[:, 0:128]
         rows[pl.ds(2 * jp + 1, 64, stride=8), :] = acc[:, 128:256]
     ps[...] = rows[...].reshape(64, 8, 128).astype(BF16)
     pr[pl.ds(b, 1)] = ps[pl.ds(b, 1)]
 
-    def scatter(k, carry):
-        p = seq_peer(k)
+    for p in seq_peers:
         send(ps.at[p], pr.at[b], p_ss, p_rs, (p, r))
-        return carry
-
-    lax.fori_loop(0, N_SEQ - 1, scatter, 0)
 
     wait_bytes(ur.at[pl.ds(0, 7)], u_rs)
     back = ur[...].astype(F32).reshape(256, 128).astype(BF16)
@@ -326,17 +364,21 @@
     outer_factor_weight, outer_output_weight, outer_product_bias,
 ):
     vm = pl.BlockSpec(memory_space=pltpu.VMEM)
+    hbm = pl.BlockSpec(memory_space=pl.ANY)
     sm = pl.BlockSpec(memory_space=pltpu.SMEM)
     V = pltpu.VMEM
     update, pair = pl.pallas_call(
         kernel,
         out_shape=(
-            jax.ShapeDtypeStruct((32, 2, 8, 64), BF16),
-            jax.ShapeDtypeStruct((8, 128), BF16),
+            V((32, 2, 8, 64), BF16),
+            V((8, 128), BF16),
         ),
-        in_specs=[vm, vm, sm, sm, vm, vm, vm, vm, vm, vm, vm],
+        in_specs=[hbm, hbm, sm] + [hbm] * 8,
         out_specs=(vm, vm),
         scratch_shapes=[
+            V((64, 8, 64), BF16), V((8, 128), BF16), pltpu.SMEM((64,), jnp.int32),
+            V((1, 64), jnp.int32), V((64, 256), BF16), V((64, 64), BF16), V((8, 128), F32),
+            V((64, 64), BF16), V((1024, 128), F32), V((1, 128), F32),
             V((8, 4, 8, 128), BF16), V((8, 4, 8, 128), BF16),
             V((4, 128), F32), V((8, 4, 128), F32),
             V((4, 128), F32), V((64, 4, 128), F32),
@@ -347,9 +389,11 @@
             V((8, 128), F32), V((8, 8, 128), F32),
             V((8, 128), F32), V((8, 8, 128), F32),
             V((4, 8, 16, 16, 256), BF16), V((16, 128, 256), BF16),
-            V((64, 1024), F32), V((512, 128), F32),
+            V((64, 1024), F32), V((512, 128), F32), V((4, 64, 1024), F32), V((4, 64, 256), F32),
+            pltpu.SemaphoreType.DMA((10,)),
         ]
-        + [pltpu.SemaphoreType.DMA] * 18,
+        + [pltpu.SemaphoreType.DMA((8,)) if n == 7 else pltpu.SemaphoreType.DMA for n in range(18)]
+        + [pltpu.SemaphoreType.REGULAR],
         compiler_params=pltpu.CompilerParams(collective_id=0, has_side_effects=True),
     )(
         alignment_rows,
@@ -359,7 +403,7 @@
         residue_present_mask.reshape(1, 64),
         attention_in_weight,
         attention_out_weight,
-        pair_bias_weight,
+        pair_bias_weight.T,
         outer_factor_weight,
         outer_output_weight,
         outer_product_bias.reshape(1, 128),

time: 56.1 us -> 45.5 us (0.81)
  Pallas kernels: 51.7 us -> 42.8 us
  local copies, waits for them, and re-layouts: 2.9 us -> 1.24 us
    pallas_call x1, Pallas kernels: 51.7 us -> 42.8 us  [local(): pl.pallas_call(kernel, out_shape=(V((32, 2, 8, 64), BF16), V((8, 128), BF...]
    unnamed x7 -> x2, local copies, waits for them, and re-layouts: 2.9 us -> 1.24 us
where the time goes in v2:
time: 45.5 us; the launch traced here: 45.3 us
  Pallas kernels  42.8 us (94%)
  between operations  1.29 us (3%)
  local copies, waits for them, and re-layouts  1.24 us (3%)
    pallas_call x1, Pallas kernels, local(): pl.pallas_call(kernel, out_shape=(V((32, 2, 8, 64), BF16), V((8, 128), BF...  42.8 us
    unnamed x2, local copies, waits for them, and re-layouts  1.24 us

profile of v2, /device:TPU:1, one launch (start us, length us, event | category | flops | bytes accessed | tf_op | source)
XLA Modules:
  0.0 45.3 jit_solution(17929312157824681125)
XLA Ops:
  1.3 42.8 %shard_map.122 = (bf16[32,2,8,64]{3,2,1,0:T(8,128)(2,1)S(1)}, bf16[8,128]{1,0:T(8,128)(2,1)S(1)}) custom-call(bf16[64,8,64]{2,1,0:T(8,128)(2,1)} %x_hbm.1, bf16[8,128]{1,0:T(8,128)(2,1)} %bitcast.9, s32[1]{0:T(128)S(6)} %copy.17.cnt_ref, s32[64]{0:T(128)} %cmc_hbm.1, s32[1,64]{1,0:T(1,128)} %bitcast.10, bf16[64,256]{1,0:T(8,128)(2,1)} %win_hbm.1, ...), custom_call_target="tpu_custom_call" | custom-call | tf_op jit(solution)/shard_map/pallas_call | solution.py:370
  44.1 0.7 %copy.15 = bf16[64,8,64]{2,1,0:T(8,128)(2,1)} copy(bf16[64,8,64]{2,1,0:T(8,128)(2,1)S(1)} %bitcast.6) | data formatting | bytes 131072
  44.8 0.6 %copy.16 = bf16[1,8,128]{2,1,0:T(8,128)(2,1)} copy(bf16[1,8,128]{2,1,0:T(8,128)(2,1)S(1)} %bitcast.7) | data formatting | bytes 4096

commit v3 on v2

--- a/solution.py
+++ b/solution.py
@@ -52,7 +52,7 @@
     upd_ref, pair_ref,
     x_ref, pf_ref, cmc_ref, mask_ref, win_ref, wout_ref, wb_ref, wf_ref, ow_ref, ob_ref,
     xs, xr, bs, br, b2s, b2r, ls, lr, rs, rr, us, ur, ps, pr, w1s, w1r, w2s, w2r,
-    tt, w4, bias2, rows, score, sums,
+    tt, w4, bias2, spare, score, sums,
     in_sems,
     x_ss, x_rs, b_ss, b_rs, b2_ss, b2_rs, l_ss, l_rs, r_ss, r_rs, u_ss, u_rs, p_ss, p_rs,
     w1_ss, w1_rs, w2_ss, w2_rs, ready,
@@ -89,7 +89,16 @@
         pl.semaphore_signal(sem, inc=1, device_id=dev, device_id_type=MESH)
 
     z_peers = [px[0] + pz[k] + pc[0] for k in far_first]
-    xc_peers = [px[k // NC] + pz[0] + pc[k % NC] for k in (4, 5, 2, 3, 6, 7, 1)]
+    xc = (4, 5, 2, 3, 6, 7, 1)
+    xc_peers = [px[k // NC] + pz[0] + pc[k % NC] for k in xc]
+    member = (bx % NX) * NC + bc
+
+    def member_at(k):
+        return ((bx + k // NC) % NX) * NC + (bc + k % NC) % NC
+
+    def member_from(k):
+        return ((bx + NX - k // NC) % NX) * NC + (bc + k % NC) % NC
+
     copies[0].start()
     copies[1].start()
     for p in z_peers:
@@ -155,14 +164,10 @@
     keep = jnp.sum(where(iota((64, 64), 0) == iota((64, 64), 1), row, 0.0), axis=1, keepdims=True)
     key_mask = where(keep == 1.0, 0.0, -1000000.0)
 
-    lane_u = iota((64, 128), 1) // 32
-    parts = []
-    for sp in range(2):
-        part = jnp.zeros((64, 128), F32)
-        for u in range(4):
-            part = where(lane_u == u, weight[2 * u + sp], part)
-        parts.append(part * keep)
-    scale_r = jnp.concatenate(parts, axis=0)
+    lane_s = iota((1, 256), 1) % 8
+    weight_lane = jnp.zeros((1, 256), F32)
+    for n in range(8):
+        weight_lane = where(lane_s == n, weight[n], weight_lane)
 
     for p in z_peers:
         send(w1s, w1r.at[bz], w1_ss, w1_rs, (p, r))
@@ -179,14 +184,12 @@
     winT = win_ref[...].astype(F32).T.astype(BF16)
     woutT = wout_ref[...].astype(F32).T.astype(BF16)
     wout2 = mm(wout_ref[...], dup).astype(BF16)
-    e_left = where(iota((64, 256), 0) == iota((64, 256), 1) // 8, 1.0, 0.0).astype(BF16)
-    e_right = where(iota((64, 128), 0) == 32 + iota((64, 128), 1) % 32, 1.0, 0.0).astype(BF16)
+    e_left = where(iota((64, 128), 0) == iota((64, 128), 1) % 32, 1.0, 0.0).astype(BF16)
+    e_right = where(iota((64, 256), 0) == 32 + iota((64, 256), 1) // 8, 1.0, 0.0).astype(BF16)
     wl = mm(wf_ref[...], e_left).astype(BF16)
     wr = mm(wf_ref[...], e_right).astype(BF16)
-    for c in range(32):
-        block = ow_ref[pl.ds(c * 32, 32), :].astype(BF16)
-        for q in range(4):
-            w4[c // 2, pl.ds(q * 32, 32), pl.ds((c % 2) * 128, 128)] = block
+    for d in range(32):
+        w4[d // 2, :, pl.ds((d % 2) * 128, 128)] = ow_ref[pl.ds(d, 32, stride=32), :].astype(BF16)
 
     wait_bytes(xr.at[pl.ds(0, 7)], x_rs)
     eye2 = where(iota((64, 128), 1) % 64 == iota((64, 128), 0), 1.0, 0.0).astype(BF16)
@@ -254,27 +257,27 @@
     oT = norm_rows(xT + uT * use_lane, 0).astype(BF16)
 
     lane_s = iota((64, 256), 1) % 8
-    left = jnp.zeros((64, 256), F32)
-    right = jnp.zeros((128, 128), F32)
-    lane_u2 = iota((128, 128), 1) // 32
+    lane_u = iota((128, 128), 1) // 32
+    right = jnp.zeros((64, 256), F32)
+    left = jnp.zeros((128, 128), F32)
     for u in range(4):
         o_rows = oT[:, u * 128 : (u + 1) * 128].T
-        zl = mm(o_rows, wl)
-        left = where(lane_s == 2 * u, zl[0:64], where(lane_s == 2 * u + 1, zl[64:128], left))
-        right = where(lane_u2 == u, mm(o_rows, wr), right)
-    right = right * scale_r
-    for p in range(8):
+        zr = mm(o_rows, wr)
+        right = where(lane_s == 2 * u, zr[0:64], where(lane_s == 2 * u + 1, zr[64:128], right))
+        left = where(lane_u == u, mm(o_rows, wl), left)
+    spare[...] = left * jnp.concatenate([keep, keep], axis=0)
+    for q in range(8):
         for sp in range(2):
-            rs[p, sp] = right[sp * 64 + p * 8 : sp * 64 + p * 8 + 8].astype(BF16)
-    rr[pl.ds(r, 1)] = rs[pl.ds(r, 1)]
-    for p in res_peers:
-        send(rs.at[p], rr.at[r], r_ss, r_rs, (b, p))
-    left = (left * keep).astype(BF16)
-    ls[...] = left
-    lr[pl.ds(r, 1)] = left[None]
-    near = (3, 5, 2, 6, 1, 7)
-    for n, k in enumerate(near):
-        send(ls, lr.at[r], l_ss, l_rs.at[n], (b, (r + k) % N_RES))
+            first = sp * 64 + (q // NC) * (NZ * NC) + q % NC
+            rs[q, sp] = spare[pl.ds(first, 8, stride=2), :].astype(BF16)
+    rr[pl.ds(member, 1)] = rs[pl.ds(member, 1)]
+    for n, p in enumerate(xc_peers):
+        send(rs.at[member_at(xc[n])], rr.at[member], r_ss, r_rs.at[n], (p, r))
+    right = (right * keep * weight_lane).astype(BF16)
+    ls[...] = right
+    lr[pl.ds(member, 1)] = right[None]
+    for n, p in enumerate(xc_peers):
+        send(ls, lr.at[member], l_ss, l_rs.at[n], (p, r))
 
     for u in range(4):
         g_rows = gT[:, u * 128 : (u + 1) * 128].T
@@ -283,57 +286,59 @@
         rows_u = where(half, z[0:64], z[64:128]).astype(BF16).astype(F32) * on
         us[:, u] = rows_u.reshape(8, 8, 128).astype(BF16)
     ur[pl.ds(r, 1)] = us[pl.ds(r, 1)]
-    wait_bytes(rr.at[pl.ds(0, 7)], r_rs)
-    packed = rr[...].astype(F32).reshape(128, 128).astype(BF16)
-    ro = iota((512, 128), 0)
-    co = iota((512, 128), 1)
-    same = (ro // 64 == co // 16) & (ro % 2 == (co // 8) % 2) & ((ro // 8) % 8 == co % 8)
-    spread_rows = mm(where(same, 1.0, 0.0).astype(BF16), packed)
-    right_all = where((ro // 2) % 4 == co // 32, spread_rows, 0.0).astype(BF16)
-
-    def times_weight(g, carry):
-        t = mm(right_all, w4[g])
-        for src in range(8):
-            for j in range(8):
-                a = src * 64 + j * 8
-                v = jnp.concatenate([t[a : a + 8, 0:128], t[a : a + 8, 128:256]], axis=0)
-                tt[j // 2, src, g, :, pl.ds((j % 2) * 128, 128)] = v.astype(BF16)
-        return carry
-
-    lax.fori_loop(0, 8, times_weight, 0, unroll=4)
-
-    before = (r + 5) % N_RES
-    after = (r + 3) % N_RES
-    wait_bytes(lr.at[0], l_rs.at[0])
-    part = lr.at[before, pl.ds(0, 32)]
-    send(part, part, l_ss, l_rs.at[6], (b, (r + 1) % N_RES))
-    wait_bytes(lr.at[0], l_rs.at[1])
-    part = lr.at[after, pl.ds(32, 32)]
-    send(part, part, l_ss, l_rs.at[7], (b, (r + 7) % N_RES))
     for p in res_peers:
         send(us.at[p], ur.at[r], u_ss, u_rs, (b, p))
-    lax.fori_loop(8, 16, times_weight, 0, unroll=4)
-
-    for n in range(2, 6):
+    fold = where(iota((128, 32), 0) % 32 == iota((128, 32), 1), 1.0, 0.0).astype(BF16)
+
+    def times_weight(srcs):
+        n = len(srcs)
+        packed = jnp.concatenate([rr[q].astype(F32).reshape(16, 128) for q in srcs], axis=0)
+        ro = iota((64 * n, 16 * n), 0)
+        co = iota((64 * n, 16 * n), 1)
+        same = (ro // 64 == co // 16) & (ro % 2 == (co // 8) % 2) & ((ro // 8) % 8 == co % 8)
+        spread_rows = mm(where(same, 1.0, 0.0).astype(BF16), packed.astype(BF16))
+        own = (iota((64 * n, 128), 0) // 2) % 4 == iota((64 * n, 128), 1) // 32
+        left_n = mm(where(own, spread_rows, 0.0).astype(BF16), fold).astype(BF16)
+
+        for g in range(16):
+            t = mm(left_n, w4[g])
+            for m, q in enumerate(srcs):
+                for i in range(8):
+                    a = m * 64 + i * 8
+                    v = jnp.concatenate([t[a : a + 8, 0:128], t[a : a + 8, 128:256]], axis=0)
+                    tt[i // 2, q, g, :, pl.ds((i % 2) * 128, 128)] = v.astype(BF16)
+
+    def products(srcs, ip):
+        acc = jnp.zeros((64, 256), F32)
+        for src in srcs:
+            acc = acc + mm(lr[src], tt[ip, src].reshape(256, 256))
+        return acc
+
+    early = [member, member_from(xc[6])]
+    late = [member_from(k) for k in xc[:6]]
+    wait_bytes(rr.at[0], r_rs.at[6])
+    times_weight(early)
+    wait_bytes(lr.at[0], l_rs.at[6])
+    for ip in range(4):
+        sums[ip] = products(early, ip)
+    for n in range(6):
+        wait_bytes(rr.at[0], r_rs.at[n])
+    times_weight(late)
+    for n in range(6):
         wait_bytes(lr.at[0], l_rs.at[n])
-    for jp in range(4):
-        acc = jnp.zeros((64, 256), F32)
-        for k in (0, 1, 7, 2, 6, 3, 5):
-            src = (r + k) % N_RES
-            acc = acc + mm(lr[src], tt[jp, src].reshape(256, 256))
-        sums[jp] = acc
-    wait_bytes(lr.at[0, pl.ds(0, 32)], l_rs.at[6])
-    wait_bytes(lr.at[0, pl.ds(0, 32)], l_rs.at[7])
-    last = (r + 4) % N_RES
-    for jp in range(4):
-        acc = sums[jp] + mm(lr[last], tt[jp, last].reshape(256, 256))
-        rows[pl.ds(2 * jp, 64, stride=8), :] = acc[:, 0:128]
-        rows[pl.ds(2 * jp + 1, 64, stride=8), :] = acc[:, 128:256]
-    ps[...] = rows[...].reshape(64, 8, 128).astype(BF16)
-    pr[pl.ds(b, 1)] = ps[pl.ds(b, 1)]
-
-    for p in seq_peers:
-        send(ps.at[p], pr.at[b], p_ss, p_rs, (p, r))
+    for ip in range(4):
+        acc = sums[ip] + products(late, ip)
+        ps[pl.ds(16 * ip, 8)] = acc[:, 0:128].reshape(8, 8, 128).astype(BF16)
+        ps[pl.ds(16 * ip + 8, 8)] = acc[:, 128:256].reshape(8, 8, 128).astype(BF16)
+    place = bz * N_RES + r
+    pr[pl.ds(place, 1)] = ps[pl.ds(place, 1)]
+    for kz in far_first + (0,):
+        for ky in far_first + (0,):
+            if kz + ky > 0:
+                qz = (bz + kz) % NZ
+                qy = (r + ky) % N_RES
+                dev = (px[0] + pz[kz] + pc[0], qy)
+                send(ps.at[qz * N_RES + qy], pr.at[place], p_ss, p_rs, dev)
 
     wait_bytes(ur.at[pl.ds(0, 7)], u_rs)
     back = ur[...].astype(F32).reshape(256, 128).astype(BF16)
@@ -343,7 +348,7 @@
     wait_bytes(w2r.at[pl.ds(0, 7)], w2_rs)
     weight_sum = jnp.sum(w2r[...], axis=0)
 
-    wait_bytes(pr.at[pl.ds(0, N_SEQ - 1)], p_rs)
+    wait_bytes(pr.at[pl.ds(0, 63)], p_rs)
     summed = jnp.sum(pr[...].astype(F32), axis=0)
     pair_ref[...] = (summed / weight_sum + ob_ref[...]).astype(BF16)
 
@@ -353,9 +358,18 @@
     wait_bytes(lr.at[pl.ds(0, 7)], l_ss)
     wait_bytes(rr.at[pl.ds(0, 7)], r_ss)
     wait_bytes(ur.at[pl.ds(0, 7)], u_ss)
-    wait_bytes(pr.at[pl.ds(0, N_SEQ - 1)], p_ss)
+    wait_bytes(pr.at[pl.ds(0, 63)], p_ss)
     wait_bytes(w1r.at[pl.ds(0, 7)], w1_ss)
     wait_bytes(w2r.at[pl.ds(0, 7)], w2_ss)
+
+
+def put_kernel(upd_in, pair_in, upd_out, pair_out, sems):
+    first = pltpu.make_async_copy(upd_in, upd_out, sems.at[0])
+    second = pltpu.make_async_copy(pair_in, pair_out, sems.at[1])
+    first.start()
+    second.start()
+    first.wait()
+    second.wait()
 
 
 def local(
@@ -388,11 +402,11 @@
             V((64, 8, 128), BF16), V((64, 8, 128), BF16),
             V((8, 128), F32), V((8, 8, 128), F32),
             V((8, 128), F32), V((8, 8, 128), F32),
-            V((4, 8, 16, 16, 256), BF16), V((16, 128, 256), BF16),
-            V((64, 1024), F32), V((512, 128), F32), V((4, 64, 1024), F32), V((4, 64, 256), F32),
+            V((4, 8, 16, 16, 256), BF16), V((16, 32, 256), BF16),
+            V((64, 1024), F32), V((128, 128), F32), V((4, 64, 1024), F32), V((4, 64, 256), F32),
             pltpu.SemaphoreType.DMA((10,)),
         ]
-        + [pltpu.SemaphoreType.DMA((8,)) if n == 7 else pltpu.SemaphoreType.DMA for n in range(18)]
+        + [pltpu.SemaphoreType.DMA((8,)) if n in (7, 9) else pltpu.SemaphoreType.DMA for n in range(18)]
         + [pltpu.SemaphoreType.REGULAR],
         compiler_params=pltpu.CompilerParams(collective_id=0, has_side_effects=True),
     )(
@@ -408,7 +422,20 @@
         outer_output_weight,
         outer_product_bias.reshape(1, 128),
     )
-    return update.reshape(64, 8, 64), pair.reshape(1, 8, 128)
+    update, pair = pl.pallas_call(
+        put_kernel,
+        out_shape=(
+            jax.ShapeDtypeStruct((64, 8, 64), BF16),
+            jax.ShapeDtypeStruct((1, 8, 128), BF16),
+        ),
+        in_specs=[vm, vm],
+        out_specs=(hbm, hbm),
+        scratch_shapes=[pltpu.SemaphoreType.DMA((2,))],
+    )(
+        pltpu.with_memory_space_constraint(update.reshape(64, 8, 64), pltpu.VMEM),
+        pltpu.with_memory_space_constraint(pair.reshape(1, 8, 128), pltpu.VMEM),
+    )
+    return update, pair
 
 
 def solution(mesh):

time: 45.5 us -> 42.5 us (0.934)
  Pallas kernels: 42.8 us -> 41 us
  local copies, waits for them, and re-layouts: 1.24 us -> 0 us
    pallas_call x1, Pallas kernels: 42.8 us -> 40.4 us  [local(): pl.pallas_call(kernel, out_shape=(V((32, 2, 8, 64), BF16), V((8, 128), BF...]
    unnamed x2 -> x0, local copies, waits for them, and re-layouts: 1.24 us -> none
    pallas_call x0 -> x1, Pallas kernels: none -> 0.68 us  [local(): pl.pallas_call(put_kernel, out_shape=(jax.ShapeDtypeStruct((64, 8, 64), B...]
where the time goes in v3:
time: 42.5 us; the launch traced here: 42.3 us
  Pallas kernels  41 us (96%)
  between operations  1.29 us (3%)
    pallas_call x1, Pallas kernels, local(): pl.pallas_call(kernel, out_shape=(V((32, 2, 8, 64), BF16), V((8, 128), BF...  40.4 us

profile of v3, /device:TPU:1, one launch (start us, length us, event | category | flops | bytes accessed | tf_op | source)
XLA Modules:
  0.0 42.3 jit_solution(575569878782129981)
XLA Ops:
  1.3 40.4 %shard_map.122 = (bf16[32,2,8,64]{3,2,1,0:T(8,128)(2,1)S(1)}, bf16[8,128]{1,0:T(8,128)(2,1)S(1)}) custom-call(bf16[64,8,64]{2,1,0:T(8,128)(2,1)} %x_hbm.1, bf16[8,128]{1,0:T(8,128)(2,1)} %bitcast.9, s32[1]{0:T(128)S(6)} %copy.13.cnt_ref, s32[64]{0:T(128)} %cmc_hbm.1, s32[1,64]{1,0:T(1,128)} %bitcast.10, bf16[64,256]{1,0:T(8,128)(2,1)} %win_hbm.1, ...), custom_call_target="tpu_custom_call" | custom-call | tf_op jit(solution)/shard_map/pallas_call | solution.py:384
  41.6 0.7 %shard_map.123 = (bf16[64,8,64]{2,1,0:T(8,128)(2,1)}, bf16[1,8,128]{2,1,0:T(8,128)(2,1)}) custom-call(bf16[64,8,64]{2,1,0:T(8,128)(2,1)S(1)} %bitcast.6, bf16[1,8,128]{2,1,0:T(8,128)(2,1)S(1)} %bitcast.7), custom_call_target="tpu_custom_call" | custom-call | tf_op jit(solution)/shard_map/pallas_call | solution.py:425

commit v4 on v3

--- a/solution.py
+++ b/solution.py
@@ -52,7 +52,7 @@
     upd_ref, pair_ref,
     x_ref, pf_ref, cmc_ref, mask_ref, win_ref, wout_ref, wb_ref, wf_ref, ow_ref, ob_ref,
     xs, xr, bs, br, b2s, b2r, ls, lr, rs, rr, us, ur, ps, pr, w1s, w1r, w2s, w2r,
-    tt, w4, bias2, spare, score, sums,
+    tt, w4, bias2, spare, gt, score, sums,
     in_sems,
     x_ss, x_rs, b_ss, b_rs, b2_ss, b2_rs, l_ss, l_rs, r_ss, r_rs, u_ss, u_rs, p_ss, p_rs,
     w1_ss, w1_rs, w2_ss, w2_rs, ready,
@@ -68,8 +68,8 @@
     pc = [(bc + k) % NC for k in range(NC)]
     seq_peers = [
         px[kx] + pz[kz] + pc[kc]
+        for kz in (4, 3, 5, 2, 6, 1, 7, 0)
         for kx in (2, 1, 3, 0)
-        for kz in (4, 3, 5, 2, 6, 1, 7, 0)
         for kc in (1, 0)
         if kx + kz + kc > 0
     ]
@@ -189,7 +189,9 @@
     wl = mm(wf_ref[...], e_left).astype(BF16)
     wr = mm(wf_ref[...], e_right).astype(BF16)
     for d in range(32):
-        w4[d // 2, :, pl.ds((d % 2) * 128, 128)] = ow_ref[pl.ds(d, 32, stride=32), :].astype(BF16)
+        block = ow_ref[pl.ds(d, 32, stride=32), :].astype(BF16)
+        for q in range(4):
+            w4[d // 2, pl.ds(q * 32, 32), pl.ds((d % 2) * 128, 128)] = block
 
     wait_bytes(xr.at[pl.ds(0, 7)], x_rs)
     eye2 = where(iota((64, 128), 1) % 64 == iota((64, 128), 0), 1.0, 0.0).astype(BF16)
@@ -249,6 +251,7 @@
             ctx.append(cx[8:16, 128:256])
         gated.append((gate[:, lanes] * jnp.concatenate(ctx, axis=0)).astype(BF16))
     gT = jnp.concatenate(gated, axis=1)
+    gt[...] = gT
     uT = mm(woutT, gT).astype(BF16).astype(F32)
     slot_lane = iota((1, 512), 1) // 64
     use_lane = jnp.zeros((1, 512), F32)
@@ -279,17 +282,6 @@
     for n, p in enumerate(xc_peers):
         send(ls, lr.at[member], l_ss, l_rs.at[n], (p, r))
 
-    for u in range(4):
-        g_rows = gT[:, u * 128 : (u + 1) * 128].T
-        z = mm(g_rows, wout2)
-        on = where(half, use[2 * u], use[2 * u + 1])
-        rows_u = where(half, z[0:64], z[64:128]).astype(BF16).astype(F32) * on
-        us[:, u] = rows_u.reshape(8, 8, 128).astype(BF16)
-    ur[pl.ds(r, 1)] = us[pl.ds(r, 1)]
-    for p in res_peers:
-        send(us.at[p], ur.at[r], u_ss, u_rs, (b, p))
-    fold = where(iota((128, 32), 0) % 32 == iota((128, 32), 1), 1.0, 0.0).astype(BF16)
-
     def times_weight(srcs):
         n = len(srcs)
         packed = jnp.concatenate([rr[q].astype(F32).reshape(16, 128) for q in srcs], axis=0)
@@ -298,7 +290,7 @@
         same = (ro // 64 == co // 16) & (ro % 2 == (co // 8) % 2) & ((ro // 8) % 8 == co % 8)
         spread_rows = mm(where(same, 1.0, 0.0).astype(BF16), packed.astype(BF16))
         own = (iota((64 * n, 128), 0) // 2) % 4 == iota((64 * n, 128), 1) // 32
-        left_n = mm(where(own, spread_rows, 0.0).astype(BF16), fold).astype(BF16)
+        left_n = where(own, spread_rows, 0.0).astype(BF16)
 
         for g in range(16):
             t = mm(left_n, w4[g])
@@ -315,30 +307,57 @@
         return acc
 
     early = [member, member_from(xc[6])]
-    late = [member_from(k) for k in xc[:6]]
+    others = [member_from(k) for k in xc[2:6] + xc[:2]]
     wait_bytes(rr.at[0], r_rs.at[6])
     times_weight(early)
     wait_bytes(lr.at[0], l_rs.at[6])
     for ip in range(4):
         sums[ip] = products(early, ip)
-    for n in range(6):
+
+    for u in range(4):
+        g_rows = gt[:, pl.ds(u * 128, 128)].T
+        z = mm(g_rows, wout2)
+        on = where(half, use[2 * u], use[2 * u + 1])
+        rows_u = where(half, z[0:64], z[64:128]).astype(BF16).astype(F32) * on
+        us[:, u] = rows_u.reshape(8, 8, 128).astype(BF16)
+    ur[pl.ds(r, 1)] = us[pl.ds(r, 1)]
+    for p in res_peers:
+        send(us.at[p], ur.at[r], u_ss, u_rs, (b, p))
+    for n in (2, 3, 4, 5, 0, 1):
         wait_bytes(rr.at[0], r_rs.at[n])
-    times_weight(late)
+    times_weight(others)
     for n in range(6):
         wait_bytes(lr.at[0], l_rs.at[n])
-    for ip in range(4):
-        acc = sums[ip] + products(late, ip)
-        ps[pl.ds(16 * ip, 8)] = acc[:, 0:128].reshape(8, 8, 128).astype(BF16)
-        ps[pl.ds(16 * ip + 8, 8)] = acc[:, 128:256].reshape(8, 8, 128).astype(BF16)
     place = bz * N_RES + r
+
+    def finish(t):
+        ip = (bz // 2 + t) % 4
+        acc = sums[ip] + products(others, ip)
+        for odd in range(2):
+            part = acc[:, 128 * odd : 128 * odd + 128].reshape(8, 8, 128)
+            ps[pl.ds((2 * ip + odd) * N_RES, 8)] = part.astype(BF16)
+
+    def scatter(qz, ky):
+        qy = (r + ky) % N_RES
+        dev = (px[0] + qz * NC + pc[0], qy)
+        send(ps.at[qz * N_RES + qy], pr.at[place], p_ss, p_rs, dev)
+
+    finish(2)
+    pair = 2 * ((bz // 2 + 2) % 4)
+    for ky in far_first + (0,):
+        for odd in range(2):
+            scatter(pair + odd, ky)
+    for t in (1, 3, 0):
+        finish(t)
     pr[pl.ds(place, 1)] = ps[pl.ds(place, 1)]
-    for kz in far_first + (0,):
-        for ky in far_first + (0,):
-            if kz + ky > 0:
-                qz = (bz + kz) % NZ
-                qy = (r + ky) % N_RES
-                dev = (px[0] + pz[kz] + pc[0], qy)
-                send(ps.at[qz * N_RES + qy], pr.at[place], p_ss, p_rs, dev)
+    for ky in far_first + (0,):
+        for t in (1, 3):
+            pair = 2 * ((bz // 2 + t) % 4)
+            for odd in range(2):
+                scatter(pair + odd, ky)
+        scatter(bz + 1 - 2 * (bz % 2), ky)
+        if ky > 0:
+            scatter(bz, ky)
 
     wait_bytes(ur.at[pl.ds(0, 7)], u_rs)
     back = ur[...].astype(F32).reshape(256, 128).astype(BF16)
@@ -402,8 +421,8 @@
             V((64, 8, 128), BF16), V((64, 8, 128), BF16),
             V((8, 128), F32), V((8, 8, 128), F32),
             V((8, 128), F32), V((8, 8, 128), F32),
-            V((4, 8, 16, 16, 256), BF16), V((16, 32, 256), BF16),
-            V((64, 1024), F32), V((128, 128), F32), V((4, 64, 1024), F32), V((4, 64, 256), F32),
+            V((4, 8, 16, 16, 256), BF16), V((16, 128, 256), BF16),
+            V((64, 1024), F32), V((128, 128), F32), V((64, 512), BF16), V((4, 64, 1024), F32), V((4, 64, 256), F32),
             pltpu.SemaphoreType.DMA((10,)),
         ]
         + [pltpu.SemaphoreType.DMA((8,)) if n in (7, 9) else pltpu.SemaphoreType.DMA for n in range(18)]

time: 42.5 us -> 41.6 us (0.979)
  Pallas kernels: 41 us -> 40.1 us
    pallas_call x1, Pallas kernels: 40.4 us -> 39.5 us  [local(): pl.pallas_call(kernel, out_shape=(V((32, 2, 8, 64), BF16), V((8, 128), BF...]
where the time goes in v4:
time: 41.6 us; the launch traced here: 41.4 us
  Pallas kernels  40.1 us (96%)
  between operations  1.29 us (3%)
    pallas_call x1, Pallas kernels, local(): pl.pallas_call(kernel, out_shape=(V((32, 2, 8, 64), BF16), V((8, 128), BF...  39.5 us

profile of v4, /device:TPU:1, one launch (start us, length us, event | category | flops | bytes accessed | tf_op | source)
XLA Modules:
  0.0 41.4 jit_solution(3629931994258645338)
XLA Ops:
  1.3 39.5 %shard_map.122 = (bf16[32,2,8,64]{3,2,1,0:T(8,128)(2,1)S(1)}, bf16[8,128]{1,0:T(8,128)(2,1)S(1)}) custom-call(bf16[64,8,64]{2,1,0:T(8,128)(2,1)} %x_hbm.1, bf16[8,128]{1,0:T(8,128)(2,1)} %bitcast.9, s32[1]{0:T(128)S(6)} %copy.13.cnt_ref, s32[64]{0:T(128)} %cmc_hbm.1, s32[1,64]{1,0:T(1,128)} %bitcast.10, bf16[64,256]{1,0:T(8,128)(2,1)} %win_hbm.1, ...), custom_call_target="tpu_custom_call" | custom-call | tf_op jit(solution)/shard_map/pallas_call | solution.py:403
  40.8 0.7 %shard_map.123 = (bf16[64,8,64]{2,1,0:T(8,128)(2,1)}, bf16[1,8,128]{2,1,0:T(8,128)(2,1)}) custom-call(bf16[64,8,64]{2,1,0:T(8,128)(2,1)S(1)} %bitcast.6, bf16[1,8,128]{2,1,0:T(8,128)(2,1)S(1)} %bitcast.7), custom_call_target="tpu_custom_call" | custom-call | tf_op jit(solution)/shard_map/pallas_call | solution.py:444

commit v5 on v4

--- a/solution.py
+++ b/solution.py
@@ -52,7 +52,7 @@
     upd_ref, pair_ref,
     x_ref, pf_ref, cmc_ref, mask_ref, win_ref, wout_ref, wb_ref, wf_ref, ow_ref, ob_ref,
     xs, xr, bs, br, b2s, b2r, ls, lr, rs, rr, us, ur, ps, pr, w1s, w1r, w2s, w2r,
-    tt, w4, bias2, spare, gt, score, sums,
+    tt, w4, bias2, spare, gt, vv, score, sums,
     in_sems,
     x_ss, x_rs, b_ss, b_rs, b2_ss, b2_rs, l_ss, l_rs, r_ss, r_rs, u_ss, u_rs, p_ss, p_rs,
     w1_ss, w1_rs, w2_ss, w2_rs, ready,
@@ -122,9 +122,6 @@
     br[pl.ds(r, 1)] = tile[None]
 
     pl.semaphore_wait(barrier, 21)
-    for p in z_peers:
-        signal(ready, (p, r))
-
     def send(src, dst, ss, rsem, dev):
         pltpu.make_async_remote_copy(
             src_ref=src, dst_ref=dst, send_sem=ss, recv_sem=rsem, device_id=dev, device_id_type=MESH
@@ -132,6 +129,8 @@
 
     for p in res_peers:
         send(bs, br.at[r], b_ss, b_rs, (b, p))
+    for p in z_peers:
+        signal(ready, (p, r))
 
     copies[2].wait()
     flat = x_ref[...].astype(F32).reshape(512, 64).astype(BF16)
@@ -206,7 +205,10 @@
     proj = mm(winT, nT)
     qT = (proj[0:64] * (1.0 / math.sqrt(8))).astype(BF16).astype(F32)
     kT = proj[64:128].astype(BF16)
-    vT = proj[128:192].astype(BF16)
+    for u in range(4):
+        for sp in range(2):
+            first = u * 128 + sp * 64
+            vv[u, pl.ds(sp * 64, 64), :] = proj[128:192, first : first + 64].astype(BF16)
     gate = jax.nn.sigmoid(proj[192:256])
 
     half2 = iota((64, 256), 1) % 128 < 64
@@ -245,8 +247,11 @@
             sc = score[u, :, pl.ds(h * 128, 256)] + bias2[:, pl.ds(h * 128, 256)]
             ex = jnp.exp(sc - jnp.max(sc, axis=0, keepdims=True))
             pb = ex * (1.0 / jnp.sum(ex, axis=0, keepdims=True))
-            p2 = jnp.concatenate([where(half2, pb, 0.0), where(half2, 0.0, pb)], axis=0)
-            cx = mm(vT[h * 8 : h * 8 + 16, lanes], p2.astype(BF16))
+            v2 = jnp.concatenate(
+                [vv[u, pl.ds(h * 8, 16), :], vv[u, pl.ds(64 + h * 8, 16), :]], axis=0
+            )
+            cx = mm(v2, pb.astype(BF16))
+            cx = where(half2[0:16], cx[0:16], cx[16:32])
             ctx.append(cx[0:8, 0:128])
             ctx.append(cx[8:16, 128:256])
         gated.append((gate[:, lanes] * jnp.concatenate(ctx, axis=0)).astype(BF16))
@@ -326,13 +331,17 @@
     for n in (2, 3, 4, 5, 0, 1):
         wait_bytes(rr.at[0], r_rs.at[n])
     times_weight(others)
-    for n in range(6):
+    for n in (4, 5, 0, 1):
+        wait_bytes(lr.at[0], l_rs.at[n])
+    for ip in range(4):
+        sums[ip] = sums[ip] + products(others[2:], ip)
+    for n in (2, 3):
         wait_bytes(lr.at[0], l_rs.at[n])
     place = bz * N_RES + r
 
     def finish(t):
         ip = (bz // 2 + t) % 4
-        acc = sums[ip] + products(others, ip)
+        acc = sums[ip] + products(others[:2], ip)
         for odd in range(2):
             part = acc[:, 128 * odd : 128 * odd + 128].reshape(8, 8, 128)
             ps[pl.ds((2 * ip + odd) * N_RES, 8)] = part.astype(BF16)
@@ -422,7 +431,8 @@
             V((8, 128), F32), V((8, 8, 128), F32),
             V((8, 128), F32), V((8, 8, 128), F32),
             V((4, 8, 16, 16, 256), BF16), V((16, 128, 256), BF16),
-            V((64, 1024), F32), V((128, 128), F32), V((64, 512), BF16), V((4, 64, 1024), F32), V((4, 64, 256), F32),
+            V((64, 1024), F32), V((128, 128), F32), V((64, 512), BF16),
+            V((4, 128, 64), BF16), V((4, 64, 1024), F32), V((4, 64, 256), F32),
             pltpu.SemaphoreType.DMA((10,)),
         ]
         + [pltpu.SemaphoreType.DMA((8,)) if n in (7, 9) else pltpu.SemaphoreType.DMA for n in range(18)]

time: 41.6 us -> 41.4 us (level)
  no operation moved by 1% of the time
where the time goes in v5:
time: 41.4 us; the launch traced here: 41.3 us
  Pallas kernels  40 us (97%)
  between operations  1.29 us (3%)
    pallas_call x1, Pallas kernels, local(): pl.pallas_call(kernel, out_shape=(V((32, 2, 8, 64), BF16), V((8, 128), BF...  39.3 us

profile of v5, /device:TPU:1, one launch (start us, length us, event | category | flops | bytes accessed | tf_op | source)
XLA Modules:
  0.0 41.3 jit_solution(10973214988212046784)
XLA Ops:
  1.3 39.3 %shard_map.122 = (bf16[32,2,8,64]{3,2,1,0:T(8,128)(2,1)S(1)}, bf16[8,128]{1,0:T(8,128)(2,1)S(1)}) custom-call(bf16[64,8,64]{2,1,0:T(8,128)(2,1)} %x_hbm.1, bf16[8,128]{1,0:T(8,128)(2,1)} %bitcast.9, s32[1]{0:T(128)S(6)} %copy.13.cnt_ref, s32[64]{0:T(128)} %cmc_hbm.1, s32[1,64]{1,0:T(1,128)} %bitcast.10, bf16[64,256]{1,0:T(8,128)(2,1)} %win_hbm.1, ...), custom_call_target="tpu_custom_call" | custom-call | tf_op jit(solution)/shard_map/pallas_call | solution.py:412
  40.6 0.7 %shard_map.123 = (bf16[64,8,64]{2,1,0:T(8,128)(2,1)}, bf16[1,8,128]{2,1,0:T(8,128)(2,1)}) custom-call(bf16[64,8,64]{2,1,0:T(8,128)(2,1)S(1)} %bitcast.6, bf16[1,8,128]{2,1,0:T(8,128)(2,1)S(1)} %bitcast.7), custom_call_target="tpu_custom_call" | custom-call | tf_op jit(solution)/shard_map/pallas_call | solution.py:454

commit v6 on v5

--- a/solution.py
+++ b/solution.py
@@ -189,8 +189,7 @@
     wr = mm(wf_ref[...], e_right).astype(BF16)
     for d in range(32):
         block = ow_ref[pl.ds(d, 32, stride=32), :].astype(BF16)
-        for q in range(4):
-            w4[d // 2, pl.ds(q * 32, 32), pl.ds((d % 2) * 128, 128)] = block
+        w4[d // 2, :, pl.ds((d % 2) * 128, 128)] = block
 
     wait_bytes(xr.at[pl.ds(0, 7)], x_rs)
     eye2 = where(iota((64, 128), 1) % 64 == iota((64, 128), 0), 1.0, 0.0).astype(BF16)
@@ -290,12 +289,14 @@
     def times_weight(srcs):
         n = len(srcs)
         packed = jnp.concatenate([rr[q].astype(F32).reshape(16, 128) for q in srcs], axis=0)
-        ro = iota((64 * n, 16 * n), 0)
-        co = iota((64 * n, 16 * n), 1)
-        same = (ro // 64 == co // 16) & (ro % 2 == (co // 8) % 2) & ((ro // 8) % 8 == co % 8)
-        spread_rows = mm(where(same, 1.0, 0.0).astype(BF16), packed.astype(BF16))
-        own = (iota((64 * n, 128), 0) // 2) % 4 == iota((64 * n, 128), 1) // 32
-        left_n = where(own, spread_rows, 0.0).astype(BF16)
+        stack = jnp.concatenate([packed[:, u * 32 : u * 32 + 32] for u in range(4)], axis=0)
+        ro = iota((64 * n, 64 * n), 0)
+        co = iota((64 * n, 64 * n), 1)
+        cu = co // (16 * n)
+        cr = co % (16 * n)
+        same = (ro // 64 == cr // 16) & (ro % 2 == (cr // 8) % 2) & ((ro // 8) % 8 == cr % 8)
+        pick = where(same & ((ro // 2) % 4 == cu), 1.0, 0.0).astype(BF16)
+        left_n = mm(pick, stack.astype(BF16)).astype(BF16)
 
         for g in range(16):
             t = mm(left_n, w4[g])
@@ -430,7 +431,7 @@
             V((64, 8, 128), BF16), V((64, 8, 128), BF16),
             V((8, 128), F32), V((8, 8, 128), F32),
             V((8, 128), F32), V((8, 8, 128), F32),
-            V((4, 8, 16, 16, 256), BF16), V((16, 128, 256), BF16),
+            V((4, 8, 16, 16, 256), BF16), V((16, 32, 256), BF16),
             V((64, 1024), F32), V((128, 128), F32), V((64, 512), BF16),
             V((4, 128, 64), BF16), V((4, 64, 1024), F32), V((4, 64, 256), F32),
             pltpu.SemaphoreType.DMA((10,)),

time: 41.4 us -> 41.4 us (level)
  no operation moved by 1% of the time
where the time goes in v6:
time: 41.4 us; the launch traced here: 41.2 us
  Pallas kernels  39.9 us (96%)
  between operations  1.29 us (3%)
    pallas_call x1, Pallas kernels, local(): pl.pallas_call(kernel, out_shape=(V((32, 2, 8, 64), BF16), V((8, 128), BF...  39.3 us

profile of v6, /device:TPU:1, one launch (start us, length us, event | category | flops | bytes accessed | tf_op | source)
XLA Modules:
  0.0 41.2 jit_solution(184351376356046346)
XLA Ops:
  1.3 39.3 %shard_map.122 = (bf16[32,2,8,64]{3,2,1,0:T(8,128)(2,1)S(1)}, bf16[8,128]{1,0:T(8,128)(2,1)S(1)}) custom-call(bf16[64,8,64]{2,1,0:T(8,128)(2,1)} %x_hbm.1, bf16[8,128]{1,0:T(8,128)(2,1)} %bitcast.9, s32[1]{0:T(128)S(6)} %copy.13.cnt_ref, s32[64]{0:T(128)} %cmc_hbm.1, s32[1,64]{1,0:T(1,128)} %bitcast.10, bf16[64,256]{1,0:T(8,128)(2,1)} %win_hbm.1, ...), custom_call_target="tpu_custom_call" | custom-call | tf_op jit(solution)/shard_map/pallas_call | solution.py:413
  40.6 0.7 %shard_map.123 = (bf16[64,8,64]{2,1,0:T(8,128)(2,1)}, bf16[1,8,128]{2,1,0:T(8,128)(2,1)}) custom-call(bf16[64,8,64]{2,1,0:T(8,128)(2,1)S(1)} %bitcast.6, bf16[1,8,128]{2,1,0:T(8,128)(2,1)S(1)} %bitcast.7), custom_call_target="tpu_custom_call" | custom-call | tf_op jit(solution)/shard_map/pallas_call | solution.py:455
